TPU v7x, 128 devices: a whole 4x4x4 slice. The times are simulated.
128 devices in a mesh: fsdp: 2 (over core), ep: 64 (over z, y, x).
Axes of the slice: x: 4, y: 4, z: 4, core: 2. Of those that a mesh axis runs over, the one named last changes fastest.
Arguments:
- grad_out: bfloat16 [8192, 1536], P(('fsdp', 'ep'))
- expert_idx: int32 [8192, 6], P(('fsdp', 'ep'))
- slot_pos: int32 [8192, 6], P(('fsdp', 'ep'))
- gates: float32 [8192, 6], P(('fsdp', 'ep'))
- x_disp: bfloat16 [64, 1024, 1536], P('ep', 'fsdp')
- h_gate: bfloat16 [64, 1024, 512], P('ep', 'fsdp')
- h_up: bfloat16 [64, 1024, 512], P('ep', 'fsdp')
- y_disp: bfloat16 [64, 1024, 1536], P('ep', 'fsdp')
- w_gate: bfloat16 [64, 1536, 512], P('ep', 'fsdp')
- w_down: bfloat16 [64, 512, 1536], P('ep', 'fsdp')
- w_up: bfloat16 [64, 1536, 512], P('ep', 'fsdp')
Outputs:
- output 1: bfloat16 [8192, 1536], P(('fsdp', 'ep'))
- output 2: float32 [8192, 6], P(('fsdp', 'ep'))
- output 3: float32 [64, 1536, 512], P('ep', 'fsdp')
- output 4: float32 [64, 512, 1536], P('ep', 'fsdp')
- output 5: float32 [64, 1536, 512], P('ep', 'fsdp')
All inputs are finite; a program needn't handle non-finite values.
Results may differ from a plain program's by a relative error of at most 0.00882546.
Values are sent between devices in bfloat16 or wider.
A program may use at most 1 GiB of HBM per device.

v0:
```python
import jax
import jax.numpy as jnp
from jax import lax
from jax.sharding import PartitionSpec as P


def expert_grads(dy_rows, gate_rows, x_rows, h_gate, h_up, y_rows, w_gate, w_down, w_up):
    g_rows = (dy_rows.astype(jnp.float32) * gate_rows[..., None]).astype(jnp.bfloat16)
    gate_pre = h_gate.astype(jnp.float32)
    up_pre = h_up.astype(jnp.float32)
    sigmoid_gate = jax.nn.sigmoid(gate_pre)
    silu_gate = gate_pre * sigmoid_gate
    act_rows = (silu_gate * up_pre).astype(jnp.bfloat16)
    d_act = jnp.einsum('erd,efd->erf', g_rows, w_down, preferred_element_type=jnp.float32)
    dh_gate = (d_act * up_pre * sigmoid_gate * (1.0 + gate_pre * (1.0 - sigmoid_gate))).astype(jnp.bfloat16)
    dh_up = (d_act * silu_gate).astype(jnp.bfloat16)
    dx_rows = (jnp.einsum('erf,edf->erd', dh_gate, w_gate, preferred_element_type=jnp.float32) + jnp.einsum('erf,edf->erd', dh_up, w_up, preferred_element_type=jnp.float32)).astype(jnp.bfloat16)
    dgate_rows = jnp.einsum('erd,erd->er', dy_rows, y_rows, preferred_element_type=jnp.float32)
    dw_gate = jnp.einsum('erd,erf->edf', x_rows, dh_gate, preferred_element_type=jnp.float32)
    dw_down = jnp.einsum('erf,erd->efd', act_rows, g_rows, preferred_element_type=jnp.float32)
    dw_up = jnp.einsum('erd,erf->edf', x_rows, dh_up, preferred_element_type=jnp.float32)
    return dx_rows, dgate_rows, dw_gate, dw_down, dw_up


def solution(mesh):
    ep_n = mesh.shape['ep']
    tok_spec = P(('fsdp', 'ep'), None)
    row_spec = P('ep', 'fsdp', None)

    def local_backward(grad_out, expert_idx, slot_pos, gates, x_disp, h_gate, h_up, y_disp, w_gate, w_down, w_up):
        tok_n, top_n = expert_idx.shape
        e_loc, rows_loc, width = x_disp.shape
        slot_cap = rows_loc // ep_n
        slots_n = e_loc * ep_n * slot_cap
        choices = tok_n * top_n
        send_row = jnp.where(slot_pos >= 0, ((expert_idx % e_loc) * ep_n + expert_idx // e_loc) * slot_cap + slot_pos, slots_n).reshape(-1)
        src_choice = jnp.full((slots_n,), choices, jnp.int32).at[send_row].set(jnp.arange(choices, dtype=jnp.int32), mode='drop')
        send_dy = jnp.take(grad_out, src_choice // top_n, axis=0, mode='fill', fill_value=0).reshape(e_loc, ep_n, slot_cap, width)
        send_gate = jnp.take(gates.reshape(-1), src_choice, mode='fill', fill_value=0).reshape(e_loc, ep_n, slot_cap)
        recv_dy = lax.all_to_all(send_dy, 'ep', 1, 1, tiled=True).reshape(e_loc, rows_loc, width)
        recv_gate = lax.all_to_all(send_gate, 'ep', 1, 1, tiled=True).reshape(e_loc, rows_loc)
        full_w_gate = lax.all_gather(w_gate, 'fsdp', axis=1, tiled=True)
        full_w_down = lax.all_gather(w_down, 'fsdp', axis=1, tiled=True)
        full_w_up = lax.all_gather(w_up, 'fsdp', axis=1, tiled=True)
        dx_rows, dgate_rows, dw_gate, dw_down, dw_up = expert_grads(recv_dy, recv_gate, x_disp, h_gate, h_up, y_disp, full_w_gate, full_w_down, full_w_up)
        back_dx = lax.all_to_all(dx_rows.reshape(e_loc, ep_n, slot_cap, width), 'ep', 1, 1, tiled=True).reshape(slots_n, width)
        back_gate = lax.all_to_all(dgate_rows.reshape(e_loc, ep_n, slot_cap), 'ep', 1, 1, tiled=True).reshape(slots_n)
        picked = jnp.take(back_dx, send_row, axis=0, mode='fill', fill_value=0).reshape(tok_n, top_n, width)
        grad_x = jnp.sum(picked.astype(jnp.float32), axis=1).astype(jnp.bfloat16)
        grad_gates = jnp.take(back_gate, send_row, mode='fill', fill_value=0).reshape(tok_n, top_n)
        grad_w_gate = lax.psum_scatter(dw_gate, 'fsdp', scatter_dimension=1, tiled=True)
        grad_w_down = lax.psum_scatter(dw_down, 'fsdp', scatter_dimension=1, tiled=True)
        grad_w_up = lax.psum_scatter(dw_up, 'fsdp', scatter_dimension=1, tiled=True)
        return grad_x, grad_gates, grad_w_gate, grad_w_down, grad_w_up

    return jax.shard_map(local_backward, mesh=mesh, in_specs=(tok_spec, tok_spec, tok_spec, tok_spec, row_spec, row_spec, row_spec, row_spec, row_spec, row_spec, row_spec), out_specs=(tok_spec, tok_spec, row_spec, row_spec, row_spec), check_vma=False)
```

profile of v0, /device:TPU:1, one launch (start us, length us, event | category | flops | bytes accessed | tf_op | source)
XLA Modules:
  0.0 156.5 jit_solution(11044716877208094121)
XLA Ops:
  9.8 2.9 %scatter_custom_fusion = s32[512]{0:T(512)S(1)} fusion(s32[384]{0:T(512)S(1)} %fusion.31, s32[384]{0:T(512)S(1)} %iota.3, s32[]{:T(128)} %constant.91.clone.1), kind=kCustom, calls=%fused_computation.61 | custom fusion | bytes 2052 | tf_op jit(solution)/shard_map/scatter | solution.py:37
  12.8 3.5 %gather_fusion.1 = f32[512]{0:T(512)S(1)} fusion(f32[384]{0:T(512)S(1)} %reshape.240, s32[1024]{0:T(1024)S(1)} %pad_clamp_fusion.1), kind=kCustom, calls=%fused_computation.1 | custom fusion | bytes 6144 | tf_op jit(solution)/shard_map/jit(_take)/gather | solution.py:39
  17.0 12.0 %all-to-all-start.1 = ((f32[1,64,8]{2,0,1:T(1,128)}), f32[1,64,8]{2,0,1:T(1,128)S(1)}, u32[]{:S(2)}, u32[]{:S(2)}) async-start(f32[1,64,8]{2,0,1:T(1,128)} %bitcast.3), calls=%async_computation.1 | async-start | bytes 65536 | tf_op jit(solution)/shard_map/all_to_all | solution.py:41
  29.8 2.1 %gather_fusion = bf16[512,1536]{1,0:T(8,128)(2,1)S(1)} fusion(bf16[64,1536]{1,0:T(8,128)(2,1)S(1)} %copy-done.1, s32[1024]{0:T(1024)S(1)} %pad_clamp_fusion.2), kind=kCustom, calls=%fused_computation | custom fusion | bytes 3147776 | tf_op jit(solution)/shard_map/jit(_take)/gather | solution.py:38
  32.0 1.3 bitcast_select_fusion
  33.3 4.0 %all-to-all-done.1 = f32[1,64,8]{2,0,1:T(1,128)S(1)} async-done(((f32[1,64,8]{2,0,1:T(1,128)}), f32[1,64,8]{2,0,1:T(1,128)S(1)}, u32[]{:S(2)}, u32[]{:S(2)}) %all-to-all-start.1) | async-done | bytes 2080 | tf_op jit(solution)/shard_map/all_to_all | solution.py:41
  37.3 5.8 %all-to-all-start = ((bf16[1,64,8,1536]{3,2,0,1:T(8,128)(2,1)}), bf16[1,64,8,1536]{3,2,0,1:T(8,128)(2,1)S(1)}, u32[]{:S(2)}, u32[]{:S(2)}) async-start(bf16[1,64,8,1536]{3,2,0,1:T(8,128)(2,1)} %bitcast_select_fusion), calls=%async_computation | async-start | bytes 3145728 | tf_op jit(solution)/shard_map/all_to_all | solution.py:40
  45.2 24.1 %all-to-all-done = bf16[1,64,8,1536]{3,2,0,1:T(8,128)(2,1)S(1)} async-done(((bf16[1,64,8,1536]{3,2,0,1:T(8,128)(2,1)}), bf16[1,64,8,1536]{3,2,0,1:T(8,128)(2,1)S(1)}, u32[]{:S(2)}, u32[]{:S(2)}) %all-to-all-start) | async-done | bytes 1572896 | tf_op jit(solution)/shard_map/all_to_all | solution.py:40
  69.3 3.8 %fusion.17 = (bf16[1,512,512]{2,1,0:T(8,128)(2,1)S(1)}, f32[1,512,512]{2,1,0:T(8,128)}) fusion(bf16[1,512,512]{2,1,0:T(8,128)(2,1)} %param.17, bf16[1,512,512]{2,1,0:T(8,128)(2,1)} %param.16, bf16[1,512,1536]{2,1,0:T(8,128)(2,1)} %all-gather.4.cloned.1.call-done, bf16[1,64,8,1536]{3,2,0,1:T(8,128)(2,1)S(1)} %all-to-all-done, f32[512]{0:T(512)S(1)} %mul.63), kind=kOutput, calls=%fused_computation.33 | convolution fusion | flops 810811392 | bytes 5769216 | tf_op jit(solution)/shard_map/erd,efd->erf/dot_general | solution.py:14
  73.9 2.6 %convolution_bitcast_fusion.2 = f32[1,1536,512]{1,2,0:T(8,128)} fusion(bf16[1,512,1536]{2,1,0:T(8,128)(2,1)S(1)} %copy-done, bf16[1,512,512]{2,1,0:T(8,128)(2,1)S(1)} %get-tuple-element.29), kind=kOutput, calls=%fused_computation.8 | convolution fusion | flops 805306368 | bytes 5242880 | tf_op jit(solution)/shard_map/erd,erf->edf/dot_general | solution.py:19
  76.6 4.1 %convolution_bitcast_fusion = f32[1,1536,512]{1,2,0:T(8,128)} fusion(bf16[1,512,1536]{2,1,0:T(8,128)(2,1)S(1)} %copy-done, f32[1,512,512]{2,1,0:T(8,128)} %get-tuple-element.30, bf16[1,512,512]{2,1,0:T(8,128)(2,1)} %param.16), kind=kOutput, calls=%fused_computation.6 | convolution fusion | flops 807141376 | bytes 6291456 | tf_op jit(solution)/shard_map/erd,erf->edf/dot_general | solution.py:21
  80.8 4.1 %convolution_bitcast_fusion.1 = f32[1,512,1536]{2,1,0:T(8,128)} fusion(bf16[1,64,8,1536]{3,2,0,1:T(8,128)(2,1)S(1)} %all-to-all-done, f32[512]{0:T(512)S(1)} %mul.63, bf16[1,512,512]{2,1,0:T(8,128)(2,1)} %param.17, bf16[1,512,512]{2,1,0:T(8,128)(2,1)} %param.16), kind=kOutput, calls=%fused_computation.7 | convolution fusion | flops 809762816 | bytes 5769216 | tf_op jit(solution)/shard_map/erf,erd->efd/dot_general | solution.py:20
  85.0 1.9 %fusion.1 = f32[512]{0:T(512)S(1)} fusion(bf16[1,512,1536]{2,1,0:T(8,128)(2,1)} %param.18, bf16[1,64,8,1536]{3,2,0,1:T(8,128)(2,1)S(1)} %all-to-all-done), kind=kLoop, calls=%fused_computation.12 | loop fusion | flops 3145216 | bytes 3147776 | tf_op jit(solution)/shard_map/erd,erd->er/dot_general | solution.py:18
  87.6 5.0 %all-to-all-start.3 = ((f32[1,64,8]{2,0,1:T(1,128)}), f32[1,64,8]{2,0,1:T(1,128)S(1)}, u32[]{:S(2)}, u32[]{:S(2)}) async-start(f32[1,64,8]{2,0,1:T(1,128)} %bitcast.16), calls=%async_computation.3 | async-start | bytes 65536 | tf_op jit(solution)/shard_map/all_to_all | solution.py:47
  92.7 4.3 %fusion.8 = f32[512,1536]{1,0:T(8,128)} fusion(bf16[1,1536,512]{2,1,0:T(8,128)(2,1)} %all-gather.6.cloned.1.call-done, bf16[1,512,512]{2,1,0:T(8,128)(2,1)} %copy-done.2), kind=kOutput, calls=%fused_computation.20 | convolution fusion | flops 805306368 | bytes 5242880 | tf_op jit(solution)/shard_map/erf,edf->erd/dot_general | solution.py:17
  97.0 4.5 %fusion.3 = bf16[1,64,8,1536]{3,2,0,1:T(8,128)(2,1)} fusion(f32[512,1536]{1,0:T(8,128)} %fusion.8, bf16[1,1536,512]{2,1,0:T(8,128)(2,1)} %all-gather.8.cloned.1.call-done, f32[1,512,512]{2,1,0:T(8,128)S(1)} %copy-done.4, bf16[1,512,512]{2,1,0:T(8,128)(2,1)S(1)} %copy-done.3), kind=kOutput, calls=%fused_computation.14 | convolution fusion | flops 808714240 | bytes 7864320 | tf_op jit(solution)/shard_map/erf,edf->erd/dot_general | solution.py:17
  101.6 9.6 %all-to-all-start.2 = ((bf16[1,64,8,1536]{3,2,0,1:T(8,128)(2,1)}), bf16[1,64,8,1536]{3,2,0,1:T(8,128)(2,1)S(1)}, u32[]{:S(2)}, u32[]{:S(2)}) async-start(bf16[1,64,8,1536]{3,2,0,1:T(8,128)(2,1)} %fusion.3), calls=%async_computation.2 | async-start | bytes 3145728 | tf_op jit(solution)/shard_map/all_to_all | solution.py:46
  112.0 2.8 %gather_fusion.3 = f32[384]{0:T(512)S(1)} fusion(f32[512]{0:T(512)S(1)} %reshape.251, s32[1024]{0:T(1024)S(1)} %pad_clamp_fusion), kind=kCustom, calls=%fused_computation.3 | custom fusion | bytes 4608 | tf_op jit(solution)/shard_map/jit(_take)/gather | solution.py:50
  115.8 21.3 %all-to-all-done.2 = bf16[1,64,8,1536]{3,2,0,1:T(8,128)(2,1)S(1)} async-done(((bf16[1,64,8,1536]{3,2,0,1:T(8,128)(2,1)}), bf16[1,64,8,1536]{3,2,0,1:T(8,128)(2,1)S(1)}, u32[]{:S(2)}, u32[]{:S(2)}) %all-to-all-start.2) | async-done | bytes 1572896 | tf_op jit(solution)/shard_map/all_to_all | solution.py:46
  137.0 2.8 %gather_fusion.2 = bf16[384,1536]{1,0:T(8,128)(2,1)} fusion(bf16[512,1536]{1,0:T(8,128)(2,1)S(1)} %bitcast.72, s32[1024]{0:T(1024)S(1)} %pad_clamp_fusion), kind=kCustom, calls=%fused_computation.2 | custom fusion | bytes 2360832 | tf_op jit(solution)/shard_map/jit(_take)/gather | solution.py:48
  139.8 2.2 %gather.26 = bf16[64,6,1536]{2,1,0:T(8,128)(2,1)S(1)} reshape(bf16[384,1536]{1,0:T(8,128)(2,1)} %gather_fusion.2) | data formatting | bytes 2359296 | tf_op jit(solution)/shard_map/jit(_take)/gather | solution.py:48
  142.1 1.5 select_reduce_fusion
  143.6 3.0 %copy.49 = f32[1,768,512]{2,1,0:T(8,128)} copy(f32[1,768,512]{1,2,0:T(8,128)} %reduce-scatter.4.cloned.1.call-done) | data formatting | bytes 3145728
  146.6 3.0 %copy.50 = f32[1,768,512]{2,1,0:T(8,128)} copy(f32[1,768,512]{1,2,0:T(8,128)} %reduce-scatter.8.cloned.1.call-done) | data formatting | bytes 3145728
  (54 shorter events, 9.7 us)
Async XLA Ops:
  7.2 66.8 %copy-start = (bf16[1,512,1536]{2,1,0:T(8,128)(2,1)S(1)}, bf16[1,512,1536]{2,1,0:T(8,128)(2,1)}, u32[]{:S(2)}) copy-start(bf16[1,512,1536]{2,1,0:T(8,128)(2,1)} %param.15) | copy-start | bytes 4718596
  7.2 62.1 %all-gather.4.cloned.1.call-start = ((), (), s32[]{:S(2)}) async-start(), calls=%async_computation.7 | async-start | bytes 2359296 | tf_op jit(solution)/shard_map/all_gather | solution.py:43
  8.7 21.1 %copy-start.1 = (bf16[64,1536]{1,0:T(8,128)(2,1)S(1)}, bf16[64,1536]{1,0:T(8,128)(2,1)}, u32[]{:S(2)}) copy-start(bf16[64,1536]{1,0:T(8,128)(2,1)} %param.11) | copy-start | bytes 589828
  17.0 20.3 %all-to-all-start.1 = ((f32[1,64,8]{2,0,1:T(1,128)}), f32[1,64,8]{2,0,1:T(1,128)S(1)}, u32[]{:S(2)}, u32[]{:S(2)}) async-start(f32[1,64,8]{2,0,1:T(1,128)} %bitcast.3), calls=%async_computation.1 | async-start | bytes 65536 | tf_op jit(solution)/shard_map/all_to_all | solution.py:41
  28.9 63.7 %all-gather.6.cloned.1.call-start = ((), (), s32[]{:S(2)}) async-start(), calls=%async_computation.8 | async-start | bytes 2359296 | tf_op jit(solution)/shard_map/all_gather | solution.py:42
  37.3 32.0 %all-to-all-start = ((bf16[1,64,8,1536]{3,2,0,1:T(8,128)(2,1)}), bf16[1,64,8,1536]{3,2,0,1:T(8,128)(2,1)S(1)}, u32[]{:S(2)}, u32[]{:S(2)}) async-start(bf16[1,64,8,1536]{3,2,0,1:T(8,128)(2,1)} %bitcast_select_fusion), calls=%async_computation | async-start | bytes 3145728 | tf_op jit(solution)/shard_map/all_to_all | solution.py:40
  43.1 53.9 %all-gather.8.cloned.1.call-start = ((), (), s32[]{:S(2)}) async-start(), calls=%async_computation.9 | async-start | bytes 2359296 | tf_op jit(solution)/shard_map/all_gather | solution.py:44
  43.8 99.8 %reduce-scatter.4.cloned.1.call-start = ((), (), s32[]{:S(2)}) async-start(), calls=%async_computation.10 | async-start | bytes 4718592 | tf_op jit(solution)/shard_map/reduce_scatter | solution.py:51
  73.1 0.8 copy-start.2
  76.6 70.0 %reduce-scatter.8.cloned.1.call-start = ((), (), s32[]{:S(2)}) async-start(), calls=%async_computation.12 | async-start | bytes 4718592 | tf_op jit(solution)/shard_map/reduce_scatter | solution.py:53
  80.8 68.9 %reduce-scatter.6.cloned.1.call-start = ((), (), s32[]{:S(2)}) async-start(), calls=%async_computation.11 | async-start | bytes 4718592 | tf_op jit(solution)/shard_map/reduce_scatter | solution.py:52
  87.6 14.0 %all-to-all-start.3 = ((f32[1,64,8]{2,0,1:T(1,128)}), f32[1,64,8]{2,0,1:T(1,128)S(1)}, u32[]{:S(2)}, u32[]{:S(2)}) async-start(f32[1,64,8]{2,0,1:T(1,128)} %bitcast.16), calls=%async_computation.3 | async-start | bytes 65536 | tf_op jit(solution)/shard_map/all_to_all | solution.py:47
  92.6 4.4 %copy-start.3 = (bf16[1,512,512]{2,1,0:T(8,128)(2,1)S(1)}, bf16[1,512,512]{2,1,0:T(8,128)(2,1)}, u32[]{:S(2)}) copy-start(bf16[1,512,512]{2,1,0:T(8,128)(2,1)} %param.16) | copy-start | bytes 1572868
  92.6 4.4 %copy-start.4 = (f32[1,512,512]{2,1,0:T(8,128)S(1)}, f32[1,512,512]{2,1,0:T(8,128)}, u32[]{:S(2)}) copy-start(f32[1,512,512]{2,1,0:T(8,128)} %get-tuple-element.30) | copy-start | bytes 3145732
  101.6 35.5 %all-to-all-start.2 = ((bf16[1,64,8,1536]{3,2,0,1:T(8,128)(2,1)}), bf16[1,64,8,1536]{3,2,0,1:T(8,128)(2,1)S(1)}, u32[]{:S(2)}, u32[]{:S(2)}) async-start(bf16[1,64,8,1536]{3,2,0,1:T(8,128)(2,1)} %fusion.3), calls=%async_computation.2 | async-start | bytes 3145728 | tf_op jit(solution)/shard_map/all_to_all | solution.py:46
Sparse Core Ops, SparseCore 0:
  9.6 16.0 all-gather.3
  31.4 14.4 all-gather.5
  47.6 13.7 all-gather.7
  76.7 9.5 reduce-scatter.3
  88.5 14.1 reduce-scatter.7
  105.5 14.1 reduce-scatter.5
where the time goes:
time: 157 us; the launch traced here: 156 us
  waiting for transfers between devices  51.4 us (33%)
  starting transfers between devices  32.6 us (21%)
  local copies, waits for them, and re-layouts  26.9 us (17%)
  matrix products  23.6 us (15%)
  between operations  14.3 us (9%)
  other arithmetic  7.6 us (5%)
    all_to_all x1, waiting for transfers between devices, local_backward(): lax.all_to_all(send_dy, 'ep', 1, 1, tiled=True)  24.1 us
    all_to_all x1, waiting for transfers between devices, local_backward(): lax.all_to_all(dx_rows.reshape(e_loc, ep_n, slot_cap, width), 'ep', 1, 1,...  21.3 us
    all_to_all x1, starting transfers between devices, local_backward(): lax.all_to_all(send_gate, 'ep', 1, 1, tiled=True).reshape(e_loc, rows_loc)  12 us
    all_to_all x1, starting transfers between devices, local_backward(): lax.all_to_all(dx_rows.reshape(e_loc, ep_n, slot_cap, width), 'ep', 1, 1,...  9.6 us
    unnamed x13, local copies, waits for them, and re-layouts  7.64 us
    all_to_all x1, starting transfers between devices, local_backward(): lax.all_to_all(send_dy, 'ep', 1, 1, tiled=True)  5.82 us
    all_to_all x1, starting transfers between devices, local_backward(): lax.all_to_all(dgate_rows.reshape(e_loc, ep_n, slot_cap), 'ep', 1, 1, til...  5.02 us
    gather x2, local copies, waits for them, and re-layouts, local_backward(): jnp.take(back_dx, send_row, axis=0, mode='fill', fill_value=0)  5.01 us
  transfers between devices with their start and end apart: 10, of which 3 were waited for; matrix products, arithmetic and copies ran while one was open for 37% of the time, Pallas kernels for 0%

commit v1 on v0

v1 whole, which is shorter than its diff:
```python
import functools

import jax
import jax.numpy as jnp
from jax import lax
from jax.experimental import pallas as pl
from jax.experimental.pallas import tpu as pltpu
from jax.sharding import PartitionSpec as P

MESH = pl.DeviceIdType.MESH
F32 = jnp.float32
BF16 = jnp.bfloat16
PLANES = 4
PLANE_ORDER = (2, 3, 1, 0)
NT = (((1,), (1,)), ((), ()))
TN = (((0,), (0,)), ((), ()))


def layer_kernel(cfg, go, eidx, slot, gates, x_in, hg_in, hu_in, y_in, wg_in, wd_in, wu_in,
                 gx, gg, dwg_out, dwd_out, dwu_out,
                 send, recv, gsend, grecv, dxs, dxr, vs, vr,
                 xv, yv, hgv, huv, wgu, wd, onehot, gv, av, dhv,
                 pg, pd, pu, rg, rd, ru, og, od, ou,
                 load_sem, wsend_sem, wrecv_sem, fsend_sem, frecv_sem, gsend_sem, grecv_sem,
                 bsend_sem, brecv_sem, vsend_sem, vrecv_sem, psend_sem, precv_sem, out_sem):
    ep_n, top, tok_n, width, hidden, cap, ysz, xsz = cfg
    plane = ep_n // PLANES
    lanes = plane * cap
    rows_chunk = plane * cap
    half_d, half_f = width // 2, hidden // 2
    q = lax.axis_index('fsdp')
    me = lax.axis_index('ep')
    other = 1 - q
    my_plane = me // plane
    my_in = lax.rem(me, plane)

    def peer_in(o):
        oy, ox = o // xsz, lax.rem(o, xsz)
        return lax.rem(my_in // xsz + oy, ysz) * xsz + lax.rem(my_in + ox, xsz)

    barrier = pltpu.get_barrier_semaphore()

    def announce(o, c):
        pl.semaphore_signal(barrier, inc=1, device_id=(q, lax.rem(me + o, ep_n)), device_id_type=MESH)
        return c

    lax.fori_loop(1, ep_n, announce, 0)
    pl.semaphore_signal(barrier, inc=1, device_id=(other, me), device_id_type=MESH)

    loads = [
        pltpu.make_async_copy(wd_in, wd.at[pl.ds(q * half_f, half_f)], load_sem.at[0]),
        pltpu.make_async_copy(wg_in, wgu.at[pl.ds(q * half_d, half_d), pl.ds(0, hidden)], load_sem.at[1]),
        pltpu.make_async_copy(wu_in, wgu.at[pl.ds(q * half_d, half_d), pl.ds(hidden, hidden)], load_sem.at[2]),
        pltpu.make_async_copy(hg_in, hgv, load_sem.at[3]),
        pltpu.make_async_copy(hu_in, huv, load_sem.at[4]),
        pltpu.make_async_copy(y_in, yv, load_sem.at[5]),
        pltpu.make_async_copy(x_in, xv, load_sem.at[6]),
    ]
    for cp in loads:
        cp.start()

    dest = jnp.where(slot[...] >= 0, eidx[...] * cap + slot[...], ep_n * cap)
    lane_t = lax.broadcasted_iota(jnp.int32, (tok_n, lanes), 1)
    for k in range(PLANES):
        hot = jnp.zeros((tok_n, lanes), F32)
        gate = jnp.zeros((tok_n, lanes), F32)
        for j in range(top):
            hit = lane_t == dest[:, j:j + 1] - k * lanes
            hot = jnp.where(hit, 1.0, hot)
            gate = jnp.where(hit, gates[:, j:j + 1], gate)
        hot = hot.astype(BF16)
        onehot[k] = hot
        gsend[k] = jnp.sum(gate, axis=0, keepdims=True)
        picked = lax.dot_general(hot, go[...], TN, preferred_element_type=F32)
        send[pl.ds(k * plane, plane)] = picked.reshape(plane, cap, width).astype(BF16)

    pl.semaphore_wait(barrier, ep_n)

    def partner_copy(src, dst, i, ssem, rsem):
        return pltpu.make_async_remote_copy(src_ref=src, dst_ref=dst, send_sem=ssem.at[i], recv_sem=rsem.at[i],
                                            device_id=(other, me), device_id_type=MESH)

    wcopies = [
        partner_copy(wd_in, wd.at[pl.ds(q * half_f, half_f)], 0, wsend_sem, wrecv_sem),
        partner_copy(wg_in, wgu.at[pl.ds(q * half_d, half_d), pl.ds(0, hidden)], 1, wsend_sem, wrecv_sem),
        partner_copy(wu_in, wgu.at[pl.ds(q * half_d, half_d), pl.ds(hidden, hidden)], 2, wsend_sem, wrecv_sem),
    ]
    for cp in wcopies:
        cp.start()

    def row_copy(src, dst, idx, ssem, rsem):
        return pltpu.make_async_remote_copy(src_ref=src.at[idx], dst_ref=dst.at[me], send_sem=ssem,
                                            recv_sem=rsem.at[my_plane], device_id=(q, idx), device_id_type=MESH)

    def gate_copy(idx):
        return pltpu.make_async_remote_copy(src_ref=gsend.at[idx // plane], dst_ref=grecv.at[me], send_sem=gsend_sem,
                                            recv_sem=grecv_sem.at[my_plane], device_id=(q, idx), device_id_type=MESH)

    for ci, dz in enumerate(PLANE_ORDER):
        to_plane = lax.rem(my_plane + PLANES - dz, PLANES)

        def send_one(o, c, to_plane=to_plane):
            idx = to_plane * plane + peer_in(o)
            gate_copy(idx).start()
            row_copy(send, recv, idx, fsend_sem, frecv_sem).start()
            return c

        lax.fori_loop(1 if dz == 0 else 0, plane, send_one, 0)
    recv[me] = send[me]
    grecv[me] = gsend[my_plane]

    def wait_bytes(buf, n, sem):
        part = buf.at[pl.ds(0, n)]
        pltpu.make_async_copy(part, part, sem).wait()

    def wait_chunk(ci, buf, sem):
        @pl.when(ci < PLANES - 1)
        def _():
            wait_bytes(buf, plane, sem)

        @pl.when(ci == PLANES - 1)
        def _():
            wait_bytes(buf, plane - 1, sem)

    for i in (0, 1, 2):
        loads[i].wait()
        wcopies[i].wait()
    for i in (3, 4, 5):
        loads[i].wait()

    lane_c = lax.broadcasted_iota(jnp.int32, (plane, cap, lanes), 2)
    sub_c = lax.broadcasted_iota(jnp.int32, (plane, cap, lanes), 1)
    mine = lane_c == my_in * cap + sub_c

    def plane_at(ci):
        n = PLANES - 1 - ci
        dz = n + (n // 2) * (5 - 2 * n)
        return lax.rem(my_plane + dz, PLANES)

    def chunk(ci, c):
        zp = plane_at(ci)
        wait_chunk(ci, recv, frecv_sem.at[zp])
        wait_chunk(ci, grecv, grecv_sem.at[zp])
        rows = pl.ds(zp * rows_chunk, rows_chunk)
        blocks = pl.ds(zp * plane, plane)
        dy = recv[blocks].astype(F32).reshape(rows_chunk, width)
        gate3 = jnp.where(mine, jnp.broadcast_to(grecv[blocks], (plane, cap, lanes)), 0.0)
        gate = jnp.sum(gate3, axis=2, keepdims=True).reshape(rows_chunk, 1)
        g = (dy * gate).astype(BF16)
        gv[rows] = g
        val = jnp.sum(dy * yv[rows].astype(F32), axis=1, keepdims=True).reshape(plane, cap, 1)
        vs[blocks] = jnp.sum(jnp.where(mine, val, 0.0), axis=1, keepdims=True)
        da = lax.dot_general(g, wd[...], NT, preferred_element_type=F32)
        h1 = hgv[rows].astype(F32)
        h3 = huv[rows].astype(F32)
        sg = jax.nn.sigmoid(h1)
        silu = h1 * sg
        av[rows] = jnp.where(gate > 0.0, silu * h3, 0.0).astype(BF16)
        dhv[rows, pl.ds(0, hidden)] = (da * h3 * sg * (1.0 + h1 * (1.0 - sg))).astype(BF16)
        dhv[rows, pl.ds(hidden, hidden)] = (da * silu).astype(BF16)
        dx = lax.dot_general(dhv[rows], wgu[...], NT, preferred_element_type=F32)
        dxs[blocks] = dx.reshape(plane, cap, width).astype(BF16)

        def back_one(o, cc):
            idx = zp * plane + peer_in(o)

            @pl.when(jnp.logical_or(ci < PLANES - 1, o > 0))
            def _():
                row_copy(dxs, dxr, idx, bsend_sem, brecv_sem).start()
                row_copy(vs, vr, idx, vsend_sem, vrecv_sem).start()

            return cc

        lax.fori_loop(0, plane, back_one, 0)
        return c

    lax.fori_loop(0, PLANES, chunk, 0)
    dxr[me] = dxs[me]
    vr[me] = vs[me]

    loads[6].wait()

    def in_grads(base, to_g, to_u):
        tile = 256 if half_d % 256 == 0 else half_d

        def step(i, c):
            cols = pl.ds(pl.multiple_of(base + i * tile, tile), tile)
            r = lax.dot_general(xv[:, cols], dhv[...], TN, preferred_element_type=F32)
            to_g[pl.ds(i * tile, tile)] = r[:, :hidden]
            to_u[pl.ds(i * tile, tile)] = r[:, hidden:]
            return c

        lax.fori_loop(0, half_d // tile, step, 0)

    def out_grads(base, to_d):
        cols = pl.ds(pl.multiple_of(base, half_f), half_f)
        to_d[...] = lax.dot_general(av[:, cols], gv[...], TN, preferred_element_type=F32)

    in_grads(other * half_d, pg, pu)
    pcopies = [partner_copy(pg, rg, 0, psend_sem, precv_sem), partner_copy(pu, ru, 1, psend_sem, precv_sem)]
    pcopies[0].start()
    pcopies[1].start()
    out_grads(other * half_f, pd)
    pcopies.append(partner_copy(pd, rd, 2, psend_sem, precv_sem))
    pcopies[2].start()
    in_grads(q * half_d, og, ou)
    out_grads(q * half_f, od)
    outs = []
    for i, (mine_ref, got, out) in enumerate(((og, rg, dwg_out), (ou, ru, dwu_out), (od, rd, dwd_out))):
        pcopies[i].wait()
        mine_ref[...] += got[...]
        cp = pltpu.make_async_copy(mine_ref, out, out_sem.at[i])
        cp.start()
        outs.append(cp)

    acc = jnp.zeros((tok_n, width), F32)
    vals = [jnp.zeros((tok_n, lanes), F32) for _ in range(top)]
    for ci, dz in enumerate(PLANE_ORDER):
        zp = lax.rem(my_plane + PLANES - dz, PLANES)
        n = plane - 1 if dz == 0 else plane
        wait_bytes(dxr, n, brecv_sem.at[zp])
        wait_bytes(vr, n, vrecv_sem.at[zp])
        blocks = pl.ds(zp * plane, plane)
        part = dxr[blocks].astype(F32).reshape(rows_chunk, width).astype(BF16)
        acc = acc + jnp.dot(onehot[zp], part, preferred_element_type=F32)
        back = jnp.sum(vr[blocks], axis=0)
        for j in range(top):
            hit = lane_t == dest[:, j:j + 1] - zp * lanes
            vals[j] = jnp.where(hit, back, vals[j])
    gx[...] = acc.astype(BF16)
    lane_k = lax.broadcasted_iota(jnp.int32, (tok_n, top), 1)
    gates_out = jnp.zeros((tok_n, top), F32)
    for j in range(top):
        gates_out = jnp.where(lane_k == j, jnp.sum(vals[j], axis=1, keepdims=True), gates_out)
    gg[...] = gates_out

    def wait_sent(buf, n, sem):
        part = buf.at[pl.ds(0, n)]
        pltpu.make_async_copy(part, part, sem).wait()

    wait_sent(send, ep_n - 1, fsend_sem)
    wait_sent(grecv, ep_n - 1, gsend_sem)
    wait_sent(dxs, ep_n - 1, bsend_sem)
    wait_sent(vs, ep_n - 1, vsend_sem)
    for cp in outs:
        cp.wait()


def solution(mesh):
    ep_n = mesh.shape['ep']
    tok_spec = P(('fsdp', 'ep'), None)
    row_spec = P('ep', 'fsdp', None)

    def local_backward(grad_out, expert_idx, slot_pos, gates, x_disp, h_gate, h_up, y_disp, w_gate, w_down, w_up):
        tok_n, top = expert_idx.shape
        _, rows, width = x_disp.shape
        hidden = h_gate.shape[2]
        cap = rows // ep_n
        plane = ep_n // PLANES
        ysz = 4 if plane == 16 else 2
        xsz = plane // ysz
        lanes = plane * cap
        half_d, half_f = width // 2, hidden // 2
        cfg = (ep_n, top, tok_n, width, hidden, cap, ysz, xsz)
        vmem = pl.BlockSpec(memory_space=pltpu.VMEM)
        hbm = pl.BlockSpec(memory_space=pl.ANY)
        dma = pltpu.SemaphoreType.DMA
        rows_buf = pltpu.VMEM((ep_n, cap, width), BF16)
        gate_buf = pltpu.VMEM((ep_n, 1, lanes), F32)
        in_part = pltpu.VMEM((half_d, hidden), F32)
        out_part = pltpu.VMEM((half_f, width), F32)
        outs = pl.pallas_call(
            functools.partial(layer_kernel, cfg),
            out_shape=[
                jax.ShapeDtypeStruct((tok_n, width), BF16),
                jax.ShapeDtypeStruct((tok_n, top), F32),
                jax.ShapeDtypeStruct((half_d, hidden), F32),
                jax.ShapeDtypeStruct((half_f, width), F32),
                jax.ShapeDtypeStruct((half_d, hidden), F32),
            ],
            in_specs=[vmem] * 4 + [hbm] * 7,
            out_specs=[vmem] * 2 + [hbm] * 3,
            scratch_shapes=[
                rows_buf, rows_buf, pltpu.VMEM((PLANES, 1, lanes), F32), gate_buf, rows_buf, rows_buf, gate_buf, gate_buf,
                pltpu.VMEM((rows, width), BF16), pltpu.VMEM((rows, width), BF16),
                pltpu.VMEM((rows, hidden), BF16), pltpu.VMEM((rows, hidden), BF16),
                pltpu.VMEM((width, 2 * hidden), BF16), pltpu.VMEM((hidden, width), BF16),
                pltpu.VMEM((PLANES, tok_n, lanes), BF16),
                pltpu.VMEM((rows, width), BF16), pltpu.VMEM((rows, hidden), BF16), pltpu.VMEM((rows, 2 * hidden), BF16),
                in_part, out_part, in_part, in_part, out_part, in_part, in_part, out_part, in_part,
                dma((7,)), dma((3,)), dma((3,)), dma, dma((PLANES,)), dma, dma((PLANES,)),
                dma, dma((PLANES,)), dma, dma((PLANES,)), dma((3,)), dma((3,)), dma((3,)),
            ],
            compiler_params=pltpu.CompilerParams(collective_id=0, has_side_effects=True, vmem_limit_bytes=60 * 1024 * 1024),
            name='layer',
        )(grad_out, expert_idx, slot_pos, gates, x_disp[0], h_gate[0], h_up[0], y_disp[0], w_gate[0], w_down[0], w_up[0])
        gx, gg, dwg, dwd, dwu = outs
        return gx, gg, dwg[None], dwd[None], dwu[None]

    return jax.shard_map(local_backward, mesh=mesh, in_specs=(tok_spec, tok_spec, tok_spec, tok_spec, row_spec, row_spec, row_spec, row_spec, row_spec, row_spec, row_spec), out_specs=(tok_spec, tok_spec, row_spec, row_spec, row_spec), check_vma=False)
```

time: 157 us -> 76.5 us (0.49)
  the two profiles are of different devices: /device:TPU:1 before, /device:TPU:3 now
where the time goes in v1:
time: 76.5 us; the launch traced here: 76.2 us
  Pallas kernels  62.4 us (82%)
  local copies, waits for them, and re-layouts  13.1 us (17%)
    pallas_call x1, Pallas kernels, local_backward(): pl.pallas_call(functools.partial(layer_kernel, cfg), out_shape=[jax.Shape...  62.4 us
    unnamed x12, local copies, waits for them, and re-layouts  13.1 us

profile of v1, /device:TPU:3, one launch (start us, length us, event | category | flops | bytes accessed | tf_op | source)
XLA Modules:
  0.0 76.2 jit_solution(3756219557044056517)
XLA Ops:
  0.6 1.4 %copy.16.eidx = s32[64,6]{1,0:T(8,128)} copy(s32[64,6]{0,1:T(8,128)} %param.12) | data formatting | bytes 3072 | tf_op args[1]
  2.0 1.4 %copy.17.slot = s32[64,6]{1,0:T(8,128)} copy(s32[64,6]{0,1:T(8,128)} %param.13) | data formatting | bytes 3072 | tf_op args[2]
  3.4 1.4 %copy.18.gates = f32[64,6]{1,0:T(8,128)} copy(f32[64,6]{0,1:T(8,128)} %param.14) | data formatting | bytes 3072 | tf_op args[3]
  4.8 62.4 %layer.1 = (bf16[64,1536]{1,0:T(8,128)(2,1)}, f32[64,6]{1,0:T(8,128)}, f32[768,512]{1,0:T(8,128)}, f32[256,1536]{1,0:T(8,128)}, f32[768,512]{1,0:T(8,128)}) custom-call(bf16[64,1536]{1,0:T(8,128)(2,1)} %go.1, s32[64,6]{1,0:T(8,128)} %copy.16.eidx, s32[64,6]{1,0:T(8,128)} %copy.17.slot, f32[64,6]{1,0:T(8,128)} %copy.18.gates, bf16[512,1536]{1,0:T(8,128)(2,1)} %bitcast.13, ...), custom_call_target="tpu_custom_call" | custom-call | tf_op jit(solution)/shard_map/layer/pallas_call | solution.py:272
  67.2 1.4 %copy.19 = f32[64,6]{0,1:T(8,128)} copy(f32[64,6]{1,0:T(8,128)} %get-tuple-element.16) | data formatting | bytes 3072
  68.6 1.6 %copy.24 = bf16[64,1536]{1,0:T(8,128)(2,1)} copy(bf16[64,1536]{1,0:T(8,128)(2,1)} %get-tuple-element.25) | data formatting | bytes 393216
  70.3 0.0 copy-start.1
  70.3 2.8 %copy.25 = f32[1,768,512]{2,1,0:T(8,128)} copy(f32[1,768,512]{2,1,0:T(8,128)} %bitcast.12) | data formatting | bytes 3145728
  73.0 0.0 copy-done.1
  73.0 0.0 copy-start
  73.1 1.1 %copy.26 = f32[1,256,1536]{2,1,0:T(8,128)} copy(f32[1,256,1536]{2,1,0:T(8,128)S(1)} %bitcast.11) | data formatting | bytes 3145728
  74.2 0.8 %copy-done = f32[768,512]{1,0:T(8,128)S(1)} copy-done((f32[768,512]{1,0:T(8,128)S(1)}, f32[768,512]{1,0:T(8,128)}, u32[]{:S(2)}) %copy-start) | copy-done | bytes 1572888
  75.0 1.1 %copy.27 = f32[1,768,512]{2,1,0:T(8,128)} copy(f32[1,768,512]{2,1,0:T(8,128)S(1)} %bitcast.10) | data formatting | bytes 3145728
Async XLA Ops:
  70.3 2.8 %copy-start.1 = (f32[256,1536]{1,0:T(8,128)S(1)}, f32[256,1536]{1,0:T(8,128)}, u32[]{:S(2)}) copy-start(f32[256,1536]{1,0:T(8,128)} %get-tuple-element.13) | copy-start | bytes 4718596
  73.0 2.0 %copy-start = (f32[768,512]{1,0:T(8,128)S(1)}, f32[768,512]{1,0:T(8,128)}, u32[]{:S(2)}) copy-start(f32[768,512]{1,0:T(8,128)} %get-tuple-element.14) | copy-start | bytes 4718596

commit v2 on v1

--- a/solution.py
+++ b/solution.py
@@ -11,18 +11,18 @@
 F32 = jnp.float32
 BF16 = jnp.bfloat16
 PLANES = 4
-PLANE_ORDER = (2, 3, 1, 0)
+PLANE_ORDER = (1, 3, 2, 0)
 NT = (((1,), (1,)), ((), ()))
 TN = (((0,), (0,)), ((), ()))
 
 
-def layer_kernel(cfg, go, eidx, slot, gates, x_in, hg_in, hu_in, y_in, wg_in, wd_in, wu_in,
-                 gx, gg, dwg_out, dwd_out, dwu_out,
-                 send, recv, gsend, grecv, dxs, dxr, vs, vr,
+def layer_kernel(cfg, go_in, eidx_in, slot_in, gates_in, x_in, hg_in, hu_in, y_in, wg_in, wd_in, wu_in,
+                 gx, gg, og, od, ou,
+                 go, eidx, slot, gates, send, recv, gsend, grecv, dxs, dxr, vs, vr,
                  xv, yv, hgv, huv, wgu, wd, onehot, gv, av, dhv,
-                 pg, pd, pu, rg, rd, ru, og, od, ou,
+                 pg, pd, pu, rg, rd, ru,
                  load_sem, wsend_sem, wrecv_sem, fsend_sem, frecv_sem, gsend_sem, grecv_sem,
-                 bsend_sem, brecv_sem, vsend_sem, vrecv_sem, psend_sem, precv_sem, out_sem):
+                 bsend_sem, brecv_sem, vsend_sem, vrecv_sem, psend_sem, precv_sem):
     ep_n, top, tok_n, width, hidden, cap, ysz, xsz = cfg
     plane = ep_n // PLANES
     lanes = plane * cap
@@ -35,7 +35,9 @@
     my_in = lax.rem(me, plane)
 
     def peer_in(o):
-        oy, ox = o // xsz, lax.rem(o, xsz)
+        half, i = o // (plane // 2), lax.rem(o, plane // 2)
+        oy = i // (xsz // 2)
+        ox = 2 * lax.rem(i, xsz // 2) + lax.rem(oy + half, 2)
         return lax.rem(my_in // xsz + oy, ysz) * xsz + lax.rem(my_in + ox, xsz)
 
     barrier = pltpu.get_barrier_semaphore()
@@ -47,6 +49,12 @@
     lax.fori_loop(1, ep_n, announce, 0)
     pl.semaphore_signal(barrier, inc=1, device_id=(other, me), device_id_type=MESH)
 
+    small = [
+        pltpu.make_async_copy(src, dst, load_sem.at[7 + i])
+        for i, (src, dst) in enumerate(((eidx_in, eidx), (slot_in, slot), (gates_in, gates), (go_in, go)))
+    ]
+    for cp in small:
+        cp.start()
     loads = [
         pltpu.make_async_copy(wd_in, wd.at[pl.ds(q * half_f, half_f)], load_sem.at[0]),
         pltpu.make_async_copy(wg_in, wgu.at[pl.ds(q * half_d, half_d), pl.ds(0, hidden)], load_sem.at[1]),
@@ -59,19 +67,23 @@
     for cp in loads:
         cp.start()
 
+    for cp in small:
+        cp.wait()
     dest = jnp.where(slot[...] >= 0, eidx[...] * cap + slot[...], ep_n * cap)
-    lane_t = lax.broadcasted_iota(jnp.int32, (tok_n, lanes), 1)
+    slot_s = lax.broadcasted_iota(jnp.int32, (lanes, tok_n), 0)
+    diag = lax.broadcasted_iota(jnp.int32, (lanes, lanes), 0) == lax.broadcasted_iota(jnp.int32, (lanes, lanes), 1)
     for k in range(PLANES):
-        hot = jnp.zeros((tok_n, lanes), F32)
-        gate = jnp.zeros((tok_n, lanes), F32)
+        hot = jnp.zeros((lanes, tok_n), F32)
+        gate = jnp.zeros((lanes, tok_n), F32)
         for j in range(top):
-            hit = lane_t == dest[:, j:j + 1] - k * lanes
+            hit = slot_s == dest[j:j + 1, :] - k * lanes
             hot = jnp.where(hit, 1.0, hot)
-            gate = jnp.where(hit, gates[:, j:j + 1], gate)
+            gate = jnp.where(hit, gates[j:j + 1, :], gate)
         hot = hot.astype(BF16)
         onehot[k] = hot
-        gsend[k] = jnp.sum(gate, axis=0, keepdims=True)
-        picked = lax.dot_general(hot, go[...], TN, preferred_element_type=F32)
+        gate_col = jnp.sum(gate, axis=1, keepdims=True)
+        gsend[k] = jnp.sum(jnp.where(diag, gate_col, 0.0), axis=0, keepdims=True)
+        picked = jnp.dot(hot, go[...], preferred_element_type=F32)
         send[pl.ds(k * plane, plane)] = picked.reshape(plane, cap, width).astype(BF16)
 
     pl.semaphore_wait(barrier, ep_n)
@@ -96,22 +108,38 @@
         return pltpu.make_async_remote_copy(src_ref=gsend.at[idx // plane], dst_ref=grecv.at[me], send_sem=gsend_sem,
                                             recv_sem=grecv_sem.at[my_plane], device_id=(q, idx), device_id_type=MESH)
 
-    for ci, dz in enumerate(PLANE_ORDER):
-        to_plane = lax.rem(my_plane + PLANES - dz, PLANES)
-
-        def send_one(o, c, to_plane=to_plane):
-            idx = to_plane * plane + peer_in(o)
-            gate_copy(idx).start()
-            row_copy(send, recv, idx, fsend_sem, frecv_sem).start()
-            return c
-
-        lax.fori_loop(1 if dz == 0 else 0, plane, send_one, 0)
-    recv[me] = send[me]
-    grecv[me] = gsend[my_plane]
-
     def wait_bytes(buf, n, sem):
         part = buf.at[pl.ds(0, n)]
         pltpu.make_async_copy(part, part, sem).wait()
+
+    def send_part(part, lo, hi, skip_own):
+        first, second = PLANE_ORDER[2 * (part // 2)], PLANE_ORDER[2 * (part // 2) + 1]
+
+        def send_one(o, c):
+            for dz in (first, second):
+                idx = lax.rem(my_plane + PLANES - dz, PLANES) * plane + peer_in(o)
+
+                def go_now():
+                    gate_copy(idx).start()
+                    row_copy(send, recv, idx, fsend_sem.at[part], frecv_sem).start()
+
+                if dz == 0 and skip_own:
+                    pl.when(o > 0)(go_now)
+                else:
+                    go_now()
+            return c
+
+        lax.fori_loop(lo, hi, send_one, 0)
+
+    half_n = plane // 2
+    send_part(0, 0, half_n, False)
+    send_part(1, half_n, plane, False)
+    recv[me] = send[me]
+    grecv[me] = gsend[my_plane]
+    wait_bytes(send, plane, fsend_sem.at[0])
+    send_part(2, 0, half_n, True)
+    wait_bytes(send, plane, fsend_sem.at[1])
+    send_part(3, half_n, plane, False)
 
     def wait_chunk(ci, buf, sem):
         @pl.when(ci < PLANES - 1)
@@ -133,7 +161,7 @@
     mine = lane_c == my_in * cap + sub_c
 
     def plane_at(ci):
-        n = PLANES - 1 - ci
+        n = lax.rem(ci + 1, PLANES)
         dz = n + (n // 2) * (5 - 2 * n)
         return lax.rem(my_plane + dz, PLANES)
 
@@ -205,16 +233,12 @@
     pcopies[2].start()
     in_grads(q * half_d, og, ou)
     out_grads(q * half_f, od)
-    outs = []
-    for i, (mine_ref, got, out) in enumerate(((og, rg, dwg_out), (ou, ru, dwu_out), (od, rd, dwd_out))):
+    for i, (mine_ref, got) in enumerate(((og, rg), (ou, ru), (od, rd))):
         pcopies[i].wait()
         mine_ref[...] += got[...]
-        cp = pltpu.make_async_copy(mine_ref, out, out_sem.at[i])
-        cp.start()
-        outs.append(cp)
 
     acc = jnp.zeros((tok_n, width), F32)
-    vals = [jnp.zeros((tok_n, lanes), F32) for _ in range(top)]
+    vals = [jnp.zeros((lanes, tok_n), F32) for _ in range(top)]
     for ci, dz in enumerate(PLANE_ORDER):
         zp = lax.rem(my_plane + PLANES - dz, PLANES)
         n = plane - 1 if dz == 0 else plane
@@ -222,27 +246,29 @@
         wait_bytes(vr, n, vrecv_sem.at[zp])
         blocks = pl.ds(zp * plane, plane)
         part = dxr[blocks].astype(F32).reshape(rows_chunk, width).astype(BF16)
-        acc = acc + jnp.dot(onehot[zp], part, preferred_element_type=F32)
-        back = jnp.sum(vr[blocks], axis=0)
+        acc = acc + lax.dot_general(onehot[zp], part, TN, preferred_element_type=F32)
+        back = jnp.sum(jnp.where(diag, jnp.sum(vr[blocks], axis=0), 0.0), axis=1, keepdims=True)
         for j in range(top):
-            hit = lane_t == dest[:, j:j + 1] - zp * lanes
+            hit = slot_s == dest[j:j + 1, :] - zp * lanes
             vals[j] = jnp.where(hit, back, vals[j])
     gx[...] = acc.astype(BF16)
-    lane_k = lax.broadcasted_iota(jnp.int32, (tok_n, top), 1)
-    gates_out = jnp.zeros((tok_n, top), F32)
     for j in range(top):
-        gates_out = jnp.where(lane_k == j, jnp.sum(vals[j], axis=1, keepdims=True), gates_out)
-    gg[...] = gates_out
-
-    def wait_sent(buf, n, sem):
-        part = buf.at[pl.ds(0, n)]
-        pltpu.make_async_copy(part, part, sem).wait()
-
-    wait_sent(send, ep_n - 1, fsend_sem)
-    wait_sent(grecv, ep_n - 1, gsend_sem)
-    wait_sent(dxs, ep_n - 1, bsend_sem)
-    wait_sent(vs, ep_n - 1, vsend_sem)
-    for cp in outs:
+        gg[j:j + 1, :] = jnp.sum(vals[j], axis=0, keepdims=True)
+
+    wait_bytes(send, plane - 1, fsend_sem.at[2])
+    wait_bytes(send, plane, fsend_sem.at[3])
+    wait_bytes(grecv, ep_n - 1, gsend_sem)
+    wait_bytes(dxs, ep_n - 1, bsend_sem)
+    wait_bytes(vs, ep_n - 1, vsend_sem)
+
+
+def write_kernel(*refs):
+    n = len(refs) // 2
+    sem = refs[-1]
+    copies = [pltpu.make_async_copy(refs[i], refs[n + i], sem.at[i]) for i in range(n)]
+    for cp in copies:
+        cp.start()
+    for cp in copies:
         cp.wait()
 
 
@@ -269,32 +295,42 @@
         gate_buf = pltpu.VMEM((ep_n, 1, lanes), F32)
         in_part = pltpu.VMEM((half_d, hidden), F32)
         out_part = pltpu.VMEM((half_f, width), F32)
+        results = [
+            jax.ShapeDtypeStruct((tok_n, width), BF16),
+            jax.ShapeDtypeStruct((top, tok_n), F32),
+            jax.ShapeDtypeStruct((half_d, hidden), F32),
+            jax.ShapeDtypeStruct((half_f, width), F32),
+            jax.ShapeDtypeStruct((half_d, hidden), F32),
+        ]
         outs = pl.pallas_call(
             functools.partial(layer_kernel, cfg),
-            out_shape=[
-                jax.ShapeDtypeStruct((tok_n, width), BF16),
-                jax.ShapeDtypeStruct((tok_n, top), F32),
-                jax.ShapeDtypeStruct((half_d, hidden), F32),
-                jax.ShapeDtypeStruct((half_f, width), F32),
-                jax.ShapeDtypeStruct((half_d, hidden), F32),
-            ],
-            in_specs=[vmem] * 4 + [hbm] * 7,
-            out_specs=[vmem] * 2 + [hbm] * 3,
+            out_shape=results,
+            in_specs=[hbm] * 11,
+            out_specs=[vmem] * 5,
             scratch_shapes=[
-                rows_buf, rows_buf, pltpu.VMEM((PLANES, 1, lanes), F32), gate_buf, rows_buf, rows_buf, gate_buf, gate_buf,
+                pltpu.VMEM((tok_n, width), BF16), pltpu.VMEM((top, tok_n), jnp.int32), pltpu.VMEM((top, tok_n), jnp.int32),
+                pltpu.VMEM((top, tok_n), F32), rows_buf, rows_buf, pltpu.VMEM((PLANES, 1, lanes), F32), gate_buf, rows_buf, rows_buf, gate_buf, gate_buf,
                 pltpu.VMEM((rows, width), BF16), pltpu.VMEM((rows, width), BF16),
                 pltpu.VMEM((rows, hidden), BF16), pltpu.VMEM((rows, hidden), BF16),
                 pltpu.VMEM((width, 2 * hidden), BF16), pltpu.VMEM((hidden, width), BF16),
-                pltpu.VMEM((PLANES, tok_n, lanes), BF16),
+                pltpu.VMEM((PLANES, lanes, tok_n), BF16),
                 pltpu.VMEM((rows, width), BF16), pltpu.VMEM((rows, hidden), BF16), pltpu.VMEM((rows, 2 * hidden), BF16),
-                in_part, out_part, in_part, in_part, out_part, in_part, in_part, out_part, in_part,
-                dma((7,)), dma((3,)), dma((3,)), dma, dma((PLANES,)), dma, dma((PLANES,)),
-                dma, dma((PLANES,)), dma, dma((PLANES,)), dma((3,)), dma((3,)), dma((3,)),
+                in_part, out_part, in_part, in_part, out_part, in_part,
+                dma((11,)), dma((3,)), dma((3,)), dma((4,)), dma((PLANES,)), dma, dma((PLANES,)),
+                dma, dma((PLANES,)), dma, dma((PLANES,)), dma((3,)), dma((3,)),
             ],
-            compiler_params=pltpu.CompilerParams(collective_id=0, has_side_effects=True, vmem_limit_bytes=60 * 1024 * 1024),
+            compiler_params=pltpu.CompilerParams(collective_id=0, has_side_effects=True, vmem_limit_bytes=44 * 1024 * 1024),
             name='layer',
-        )(grad_out, expert_idx, slot_pos, gates, x_disp[0], h_gate[0], h_up[0], y_disp[0], w_gate[0], w_down[0], w_up[0])
-        gx, gg, dwg, dwd, dwu = outs
-        return gx, gg, dwg[None], dwd[None], dwu[None]
+        )(grad_out, expert_idx.T, slot_pos.T, gates.T, x_disp[0], h_gate[0], h_up[0], y_disp[0], w_gate[0], w_down[0], w_up[0])
+        gx, gg, dwg, dwd, dwu = pl.pallas_call(
+            write_kernel,
+            out_shape=results,
+            in_specs=[vmem] * 5,
+            out_specs=[hbm] * 5,
+            scratch_shapes=[dma((5,))],
+            compiler_params=pltpu.CompilerParams(vmem_limit_bytes=8 * 1024 * 1024),
+            name='write',
+        )(*outs)
+        return gx, gg.T, dwg[None], dwd[None], dwu[None]
 
     return jax.shard_map(local_backward, mesh=mesh, in_specs=(tok_spec, tok_spec, tok_spec, tok_spec, row_spec, row_spec, row_spec, row_spec, row_spec, row_spec, row_spec), out_specs=(tok_spec, tok_spec, row_spec, row_spec, row_spec), check_vma=False)

time: 76.5 us -> 76.5 us (level)
  the two profiles are of different devices: /device:TPU:3 before, /device:TPU:97 now
where the time goes in v2:
time: 76.5 us; the launch traced here: 76 us
  Pallas kernels  65.5 us (86%)
  local copies, waits for them, and re-layouts  9.87 us (13%)
    pallas_call x1, Pallas kernels, local_backward(): pl.pallas_call(functools.partial(layer_kernel, cfg), out_shape=results, i...  63.2 us
    unnamed x20, local copies, waits for them, and re-layouts  9.87 us
    pallas_call x1, Pallas kernels, local_backward(): pl.pallas_call(write_kernel, out_shape=results, in_specs=[vmem] * 5, out_...  2.29 us

profile of v2, /device:TPU:97, one launch (start us, length us, event | category | flops | bytes accessed | tf_op | source)
XLA Modules:
  0.0 76.0 jit_solution(11336565405131923344)
XLA Ops:
  0.6 0.0 copy-start
  0.6 1.4 %copy-done = bf16[1,512,1536]{2,1,0:T(8,128)(2,1)S(1)} copy-done((bf16[1,512,1536]{2,1,0:T(8,128)(2,1)S(1)}, bf16[1,512,1536]{2,1,0:T(8,128)(2,1)}, u32[]{:S(2)}) %copy-start) | copy-done | bytes 1572888
  2.0 0.0 copy-start.1
  2.0 1.1 %copy-done.1 = bf16[1,768,512]{2,1,0:T(8,128)(2,1)S(1)} copy-done((bf16[1,768,512]{2,1,0:T(8,128)(2,1)S(1)}, bf16[1,768,512]{2,1,0:T(8,128)(2,1)}, u32[]{:S(2)}) %copy-start.1) | copy-done | bytes 786456
  3.2 0.0 copy-start.2
  3.2 1.1 %copy-done.2 = bf16[1,256,1536]{2,1,0:T(8,128)(2,1)S(1)} copy-done((bf16[1,256,1536]{2,1,0:T(8,128)(2,1)S(1)}, bf16[1,256,1536]{2,1,0:T(8,128)(2,1)}, u32[]{:S(2)}) %copy-start.2) | copy-done | bytes 786456
  4.3 0.0 copy-start.3
  4.3 1.1 %copy-done.3 = bf16[1,768,512]{2,1,0:T(8,128)(2,1)S(1)} copy-done((bf16[1,768,512]{2,1,0:T(8,128)(2,1)S(1)}, bf16[1,768,512]{2,1,0:T(8,128)(2,1)}, u32[]{:S(2)}) %copy-start.3) | copy-done | bytes 786456
  5.4 0.0 copy-start.4
  5.4 1.0 %copy-done.4 = bf16[1,512,512]{2,1,0:T(8,128)(2,1)S(1)} copy-done((bf16[1,512,512]{2,1,0:T(8,128)(2,1)S(1)}, bf16[1,512,512]{2,1,0:T(8,128)(2,1)}, u32[]{:S(2)}) %copy-start.4) | copy-done | bytes 524312
  6.5 0.0 copy-start.5
  6.5 1.0 %copy-done.5 = bf16[1,512,512]{2,1,0:T(8,128)(2,1)S(1)} copy-done((bf16[1,512,512]{2,1,0:T(8,128)(2,1)S(1)}, bf16[1,512,512]{2,1,0:T(8,128)(2,1)}, u32[]{:S(2)}) %copy-start.5) | copy-done | bytes 524312
  7.5 0.0 copy-start.6
  7.5 0.9 %copy-done.6 = bf16[64,1536]{1,0:T(8,128)(2,1)S(1)} copy-done((bf16[64,1536]{1,0:T(8,128)(2,1)S(1)}, bf16[64,1536]{1,0:T(8,128)(2,1)}, u32[]{:S(2)}) %copy-start.6) | copy-done | bytes 196632
  8.5 0.0 copy-start.7
  8.5 0.7 copy-done.7
  9.1 0.0 copy-start.8
  9.1 0.7 copy-done.8
  9.8 0.0 copy-start.9
  9.8 0.7 copy-done.9
  10.5 63.2 %layer.1 = (bf16[64,1536]{1,0:T(8,128)(2,1)S(1)}, f32[6,64]{1,0:T(8,128)S(1)}, f32[768,512]{1,0:T(8,128)S(1)}, f32[256,1536]{1,0:T(8,128)S(1)}, f32[768,512]{1,0:T(8,128)S(1)}) custom-call(bf16[64,1536]{1,0:T(8,128)(2,1)S(1)} %copy-done.6, s32[6,64]{1,0:T(8,128)S(1)} %bitcast.20, s32[6,64]{1,0:T(8,128)S(1)} %bitcast.21, f32[6,64]{1,0:T(8,128)S(1)} %bitcast.22, ...), custom_call_target="tpu_custom_call" | custom-call | tf_op jit(solution)/shard_map/layer/pallas_call | solution.py:305
  73.7 2.3 %write.1 = (bf16[64,1536]{1,0:T(8,128)(2,1)}, f32[6,64]{1,0:T(8,128)}, f32[768,512]{1,0:T(8,128)}, f32[256,1536]{1,0:T(8,128)}, f32[768,512]{1,0:T(8,128)}) custom-call(bf16[64,1536]{1,0:T(8,128)(2,1)S(1)} %get-tuple-element.15.refs_0_, f32[6,64]{1,0:T(8,128)S(1)} %get-tuple-element.16.refs_1_, f32[768,512]{1,0:T(8,128)S(1)} %get-tuple-element.17.refs_2_, ...), custom_call_target="tpu_custom_call" | custom-call | tf_op jit(solution)/shard_map/write/pallas_call | solution.py:325
Async XLA Ops:
  0.6 1.4 %copy-start = (bf16[1,512,1536]{2,1,0:T(8,128)(2,1)S(1)}, bf16[1,512,1536]{2,1,0:T(8,128)(2,1)}, u32[]{:S(2)}) copy-start(bf16[1,512,1536]{2,1,0:T(8,128)(2,1)} %param.15) | copy-start | bytes 4718596
  2.0 1.1 %copy-start.1 = (bf16[1,768,512]{2,1,0:T(8,128)(2,1)S(1)}, bf16[1,768,512]{2,1,0:T(8,128)(2,1)}, u32[]{:S(2)}) copy-start(bf16[1,768,512]{2,1,0:T(8,128)(2,1)} %param.19) | copy-start | bytes 2359300
  3.2 1.1 %copy-start.2 = (bf16[1,256,1536]{2,1,0:T(8,128)(2,1)S(1)}, bf16[1,256,1536]{2,1,0:T(8,128)(2,1)}, u32[]{:S(2)}) copy-start(bf16[1,256,1536]{2,1,0:T(8,128)(2,1)} %param.20) | copy-start | bytes 2359300
  4.3 1.1 %copy-start.3 = (bf16[1,768,512]{2,1,0:T(8,128)(2,1)S(1)}, bf16[1,768,512]{2,1,0:T(8,128)(2,1)}, u32[]{:S(2)}) copy-start(bf16[1,768,512]{2,1,0:T(8,128)(2,1)} %param.21) | copy-start | bytes 2359300
  5.4 1.0 %copy-start.4 = (bf16[1,512,512]{2,1,0:T(8,128)(2,1)S(1)}, bf16[1,512,512]{2,1,0:T(8,128)(2,1)}, u32[]{:S(2)}) copy-start(bf16[1,512,512]{2,1,0:T(8,128)(2,1)} %param.16) | copy-start | bytes 1572868
  6.5 1.0 %copy-start.5 = (bf16[1,512,512]{2,1,0:T(8,128)(2,1)S(1)}, bf16[1,512,512]{2,1,0:T(8,128)(2,1)}, u32[]{:S(2)}) copy-start(bf16[1,512,512]{2,1,0:T(8,128)(2,1)} %param.17) | copy-start | bytes 1572868
  7.5 0.9 %copy-start.6 = (bf16[64,1536]{1,0:T(8,128)(2,1)S(1)}, bf16[64,1536]{1,0:T(8,128)(2,1)}, u32[]{:S(2)}) copy-start(bf16[64,1536]{1,0:T(8,128)(2,1)} %go_in.1) | copy-start | bytes 589828
  8.5 0.7 copy-start.7
  9.1 0.7 copy-start.8
  9.8 0.7 copy-start.9

commit v3 on v2

--- a/solution.py
+++ b/solution.py
@@ -289,7 +289,7 @@
         half_d, half_f = width // 2, hidden // 2
         cfg = (ep_n, top, tok_n, width, hidden, cap, ysz, xsz)
         vmem = pl.BlockSpec(memory_space=pltpu.VMEM)
-        hbm = pl.BlockSpec(memory_space=pl.ANY)
+        hbm = pl.BlockSpec(memory_space=pltpu.HBM)
         dma = pltpu.SemaphoreType.DMA
         rows_buf = pltpu.VMEM((ep_n, cap, width), BF16)
         gate_buf = pltpu.VMEM((ep_n, 1, lanes), F32)

time: 76.5 us -> 76.5 us (level)
  no operation moved by 1% of the time
where the time goes in v3:
time: 76.5 us; the launch traced here: 76 us
  Pallas kernels  65.5 us (86%)
  local copies, waits for them, and re-layouts  9.87 us (13%)
    pallas_call x1, Pallas kernels, local_backward(): pl.pallas_call(functools.partial(layer_kernel, cfg), out_shape=results, i...  63.2 us
    unnamed x20, local copies, waits for them, and re-layouts  9.87 us
    pallas_call x1, Pallas kernels, local_backward(): pl.pallas_call(write_kernel, out_shape=results, in_specs=[vmem] * 5, out_...  2.29 us

profile of v3, /device:TPU:97, one launch (start us, length us, event | category | flops | bytes accessed | tf_op | source)
XLA Modules:
  0.0 76.0 jit_solution(11336565405131923344)
XLA Ops:
  0.6 0.0 copy-start
  0.6 1.4 %copy-done = bf16[1,512,1536]{2,1,0:T(8,128)(2,1)S(1)} copy-done((bf16[1,512,1536]{2,1,0:T(8,128)(2,1)S(1)}, bf16[1,512,1536]{2,1,0:T(8,128)(2,1)}, u32[]{:S(2)}) %copy-start) | copy-done | bytes 1572888
  2.0 0.0 copy-start.1
  2.0 1.1 %copy-done.1 = bf16[1,768,512]{2,1,0:T(8,128)(2,1)S(1)} copy-done((bf16[1,768,512]{2,1,0:T(8,128)(2,1)S(1)}, bf16[1,768,512]{2,1,0:T(8,128)(2,1)}, u32[]{:S(2)}) %copy-start.1) | copy-done | bytes 786456
  3.2 0.0 copy-start.2
  3.2 1.1 %copy-done.2 = bf16[1,256,1536]{2,1,0:T(8,128)(2,1)S(1)} copy-done((bf16[1,256,1536]{2,1,0:T(8,128)(2,1)S(1)}, bf16[1,256,1536]{2,1,0:T(8,128)(2,1)}, u32[]{:S(2)}) %copy-start.2) | copy-done | bytes 786456
  4.3 0.0 copy-start.3
  4.3 1.1 %copy-done.3 = bf16[1,768,512]{2,1,0:T(8,128)(2,1)S(1)} copy-done((bf16[1,768,512]{2,1,0:T(8,128)(2,1)S(1)}, bf16[1,768,512]{2,1,0:T(8,128)(2,1)}, u32[]{:S(2)}) %copy-start.3) | copy-done | bytes 786456
  5.4 0.0 copy-start.4
  5.4 1.0 %copy-done.4 = bf16[1,512,512]{2,1,0:T(8,128)(2,1)S(1)} copy-done((bf16[1,512,512]{2,1,0:T(8,128)(2,1)S(1)}, bf16[1,512,512]{2,1,0:T(8,128)(2,1)}, u32[]{:S(2)}) %copy-start.4) | copy-done | bytes 524312
  6.5 0.0 copy-start.5
  6.5 1.0 %copy-done.5 = bf16[1,512,512]{2,1,0:T(8,128)(2,1)S(1)} copy-done((bf16[1,512,512]{2,1,0:T(8,128)(2,1)S(1)}, bf16[1,512,512]{2,1,0:T(8,128)(2,1)}, u32[]{:S(2)}) %copy-start.5) | copy-done | bytes 524312
  7.5 0.0 copy-start.6
  7.5 0.9 %copy-done.6 = bf16[64,1536]{1,0:T(8,128)(2,1)S(1)} copy-done((bf16[64,1536]{1,0:T(8,128)(2,1)S(1)}, bf16[64,1536]{1,0:T(8,128)(2,1)}, u32[]{:S(2)}) %copy-start.6) | copy-done | bytes 196632
  8.5 0.0 copy-start.7
  8.5 0.7 copy-done.7
  9.1 0.0 copy-start.8
  9.1 0.7 copy-done.8
  9.8 0.0 copy-start.9
  9.8 0.7 copy-done.9
  10.5 63.2 %layer.1 = (bf16[64,1536]{1,0:T(8,128)(2,1)S(1)}, f32[6,64]{1,0:T(8,128)S(1)}, f32[768,512]{1,0:T(8,128)S(1)}, f32[256,1536]{1,0:T(8,128)S(1)}, f32[768,512]{1,0:T(8,128)S(1)}) custom-call(bf16[64,1536]{1,0:T(8,128)(2,1)S(1)} %copy-done.6, s32[6,64]{1,0:T(8,128)S(1)} %bitcast.20, s32[6,64]{1,0:T(8,128)S(1)} %bitcast.21, f32[6,64]{1,0:T(8,128)S(1)} %bitcast.22, ...), custom_call_target="tpu_custom_call" | custom-call | tf_op jit(solution)/shard_map/layer/pallas_call | solution.py:305
  73.7 2.3 %write.1 = (bf16[64,1536]{1,0:T(8,128)(2,1)}, f32[6,64]{1,0:T(8,128)}, f32[768,512]{1,0:T(8,128)}, f32[256,1536]{1,0:T(8,128)}, f32[768,512]{1,0:T(8,128)}) custom-call(bf16[64,1536]{1,0:T(8,128)(2,1)S(1)} %get-tuple-element.15.refs_0_, f32[6,64]{1,0:T(8,128)S(1)} %get-tuple-element.16.refs_1_, f32[768,512]{1,0:T(8,128)S(1)} %get-tuple-element.17.refs_2_, ...), custom_call_target="tpu_custom_call" | custom-call | tf_op jit(solution)/shard_map/write/pallas_call | solution.py:325
Async XLA Ops:
  0.6 1.4 %copy-start = (bf16[1,512,1536]{2,1,0:T(8,128)(2,1)S(1)}, bf16[1,512,1536]{2,1,0:T(8,128)(2,1)}, u32[]{:S(2)}) copy-start(bf16[1,512,1536]{2,1,0:T(8,128)(2,1)} %param.15) | copy-start | bytes 4718596
  2.0 1.1 %copy-start.1 = (bf16[1,768,512]{2,1,0:T(8,128)(2,1)S(1)}, bf16[1,768,512]{2,1,0:T(8,128)(2,1)}, u32[]{:S(2)}) copy-start(bf16[1,768,512]{2,1,0:T(8,128)(2,1)} %param.19) | copy-start | bytes 2359300
  3.2 1.1 %copy-start.2 = (bf16[1,256,1536]{2,1,0:T(8,128)(2,1)S(1)}, bf16[1,256,1536]{2,1,0:T(8,128)(2,1)}, u32[]{:S(2)}) copy-start(bf16[1,256,1536]{2,1,0:T(8,128)(2,1)} %param.20) | copy-start | bytes 2359300
  4.3 1.1 %copy-start.3 = (bf16[1,768,512]{2,1,0:T(8,128)(2,1)S(1)}, bf16[1,768,512]{2,1,0:T(8,128)(2,1)}, u32[]{:S(2)}) copy-start(bf16[1,768,512]{2,1,0:T(8,128)(2,1)} %param.21) | copy-start | bytes 2359300
  5.4 1.0 %copy-start.4 = (bf16[1,512,512]{2,1,0:T(8,128)(2,1)S(1)}, bf16[1,512,512]{2,1,0:T(8,128)(2,1)}, u32[]{:S(2)}) copy-start(bf16[1,512,512]{2,1,0:T(8,128)(2,1)} %param.16) | copy-start | bytes 1572868
  6.5 1.0 %copy-start.5 = (bf16[1,512,512]{2,1,0:T(8,128)(2,1)S(1)}, bf16[1,512,512]{2,1,0:T(8,128)(2,1)}, u32[]{:S(2)}) copy-start(bf16[1,512,512]{2,1,0:T(8,128)(2,1)} %param.17) | copy-start | bytes 1572868
  7.5 0.9 %copy-start.6 = (bf16[64,1536]{1,0:T(8,128)(2,1)S(1)}, bf16[64,1536]{1,0:T(8,128)(2,1)}, u32[]{:S(2)}) copy-start(bf16[64,1536]{1,0:T(8,128)(2,1)} %go_in.1) | copy-start | bytes 589828
  8.5 0.7 copy-start.7
  9.1 0.7 copy-start.8
  9.8 0.7 copy-start.9

commit v4 on v3

--- a/solution.py
+++ b/solution.py
@@ -321,7 +321,7 @@
             ],
             compiler_params=pltpu.CompilerParams(collective_id=0, has_side_effects=True, vmem_limit_bytes=44 * 1024 * 1024),
             name='layer',
-        )(grad_out, expert_idx.T, slot_pos.T, gates.T, x_disp[0], h_gate[0], h_up[0], y_disp[0], w_gate[0], w_down[0], w_up[0])
+        )(*[pltpu.with_memory_space_constraint(v, pltpu.HBM) for v in (grad_out, expert_idx.T, slot_pos.T, gates.T, x_disp[0], h_gate[0], h_up[0], y_disp[0], w_gate[0], w_down[0], w_up[0])])
         gx, gg, dwg, dwd, dwu = pl.pallas_call(
             write_kernel,
             out_shape=results,

time: 76.5 us -> 67 us (0.88)
  the two profiles are of different devices: /device:TPU:97 before, /device:TPU:49 now
where the time goes in v4:
time: 67 us; the launch traced here: 66.9 us
  Pallas kernels  66.3 us (99%)
    pallas_call x1, Pallas kernels, local_backward(): pl.pallas_call(functools.partial(layer_kernel, cfg), out_shape=results, i...  64 us
    pallas_call x1, Pallas kernels, local_backward(): pl.pallas_call(write_kernel, out_shape=results, in_specs=[vmem] * 5, out_...  2.29 us

profile of v4, /device:TPU:49, one launch (start us, length us, event | category | flops | bytes accessed | tf_op | source)
XLA Modules:
  0.0 66.9 jit_solution(11380665910154168298)
XLA Ops:
  0.6 64.0 %layer.1 = (bf16[64,1536]{1,0:T(8,128)(2,1)S(1)}, f32[6,64]{1,0:T(8,128)S(1)}, f32[768,512]{1,0:T(8,128)S(1)}, f32[256,1536]{1,0:T(8,128)S(1)}, f32[768,512]{1,0:T(8,128)S(1)}) custom-call(bf16[64,1536]{1,0:T(8,128)(2,1)} %go_in.1, s32[6,64]{1,0:T(8,128)} %bitcast.21, s32[6,64]{1,0:T(8,128)} %bitcast.22, f32[6,64]{1,0:T(8,128)} %bitcast.23, ...), custom_call_target="tpu_custom_call" | custom-call | tf_op jit(solution)/shard_map/layer/pallas_call | solution.py:305
  64.6 2.3 %write.1 = (bf16[64,1536]{1,0:T(8,128)(2,1)}, f32[6,64]{1,0:T(8,128)}, f32[768,512]{1,0:T(8,128)}, f32[256,1536]{1,0:T(8,128)}, f32[768,512]{1,0:T(8,128)}) custom-call(bf16[64,1536]{1,0:T(8,128)(2,1)S(1)} %get-tuple-element.15.refs_0_, f32[6,64]{1,0:T(8,128)S(1)} %get-tuple-element.16.refs_1_, f32[768,512]{1,0:T(8,128)S(1)} %get-tuple-element.17.refs_2_, ...), custom_call_target="tpu_custom_call" | custom-call | tf_op jit(solution)/shard_map/write/pallas_call | solution.py:325

commit v5 on v4

--- a/solution.py
+++ b/solution.py
@@ -11,19 +11,23 @@
 F32 = jnp.float32
 BF16 = jnp.bfloat16
 PLANES = 4
-PLANE_ORDER = (1, 3, 2, 0)
+ORDERS = {'near': (1, 3, 2, 0), 'far': (2, 3, 1, 0)}
 NT = (((1,), (1,)), ((), ()))
 TN = (((0,), (0,)), ((), ()))
 
 
-def layer_kernel(cfg, go_in, eidx_in, slot_in, gates_in, x_in, hg_in, hu_in, y_in, wg_in, wd_in, wu_in,
+OPT = dict(order='near', mirror=False)
+
+
+def layer_kernel(cfg, opt, go_in, eidx_in, slot_in, gates_in, x_in, hg_in, hu_in, y_in, wg_in, wd_in, wu_in,
                  gx, gg, og, od, ou,
-                 go, eidx, slot, gates, send, recv, gsend, grecv, dxs, dxr, vs, vr,
+                 go, eidx, slot, gates, send, recv, gsend, gz, grecv, dxs, dxr, vs, vr, vsum, back4,
                  xv, yv, hgv, huv, wgu, wd, onehot, gv, av, dhv,
                  pg, pd, pu, rg, rd, ru,
                  load_sem, wsend_sem, wrecv_sem, fsend_sem, frecv_sem, gsend_sem, grecv_sem,
                  bsend_sem, brecv_sem, vsend_sem, vrecv_sem, psend_sem, precv_sem):
     ep_n, top, tok_n, width, hidden, cap, ysz, xsz = cfg
+    PLANE_ORDER = ORDERS[opt['order']]
     plane = ep_n // PLANES
     lanes = plane * cap
     rows_chunk = plane * cap
@@ -38,7 +42,11 @@
         half, i = o // (plane // 2), lax.rem(o, plane // 2)
         oy = i // (xsz // 2)
         ox = 2 * lax.rem(i, xsz // 2) + lax.rem(oy + half, 2)
-        return lax.rem(my_in // xsz + oy, ysz) * xsz + lax.rem(my_in + ox, xsz)
+        my_y, my_x = my_in // xsz, lax.rem(my_in, xsz)
+        if opt['mirror']:
+            oy = oy + lax.rem(my_y, 2) * (ysz - 2 * oy)
+            ox = ox + lax.rem(my_x, 2) * (xsz - 2 * ox)
+        return lax.rem(my_y + oy, ysz) * xsz + lax.rem(my_x + ox, xsz)
 
     barrier = pltpu.get_barrier_semaphore()
 
@@ -104,9 +112,16 @@
         return pltpu.make_async_remote_copy(src_ref=src.at[idx], dst_ref=dst.at[me], send_sem=ssem,
                                             recv_sem=rsem.at[my_plane], device_id=(q, idx), device_id_type=MESH)
 
-    def gate_copy(idx):
-        return pltpu.make_async_remote_copy(src_ref=gsend.at[idx // plane], dst_ref=grecv.at[me], send_sem=gsend_sem,
-                                            recv_sem=grecv_sem.at[my_plane], device_id=(q, idx), device_id_type=MESH)
+    def line_copy(dz, src, dst, ssem, rsem):
+        zt = lax.rem(my_plane + dz, PLANES)
+        return pltpu.make_async_remote_copy(src_ref=src.at[zt], dst_ref=dst.at[my_plane], send_sem=ssem, recv_sem=rsem,
+                                            device_id=(q, zt * plane + my_in), device_id_type=MESH)
+
+    def in_plane_copy(o, src, dst, ssem, rsem):
+        to = peer_in(o)
+        part = src if len(src.shape) == 3 else src.at[to]
+        return pltpu.make_async_remote_copy(src_ref=part, dst_ref=dst.at[my_in], send_sem=ssem, recv_sem=rsem,
+                                            device_id=(q, my_plane * plane + to), device_id_type=MESH)
 
     def wait_bytes(buf, n, sem):
         part = buf.at[pl.ds(0, n)]
@@ -120,7 +135,6 @@
                 idx = lax.rem(my_plane + PLANES - dz, PLANES) * plane + peer_in(o)
 
                 def go_now():
-                    gate_copy(idx).start()
                     row_copy(send, recv, idx, fsend_sem.at[part], frecv_sem).start()
 
                 if dz == 0 and skip_own:
@@ -132,13 +146,21 @@
         lax.fori_loop(lo, hi, send_one, 0)
 
     half_n = plane // 2
+    for dz in range(1, PLANES):
+        line_copy(dz, gsend, gz, gsend_sem.at[0], grecv_sem.at[0]).start()
     send_part(0, 0, half_n, False)
+    recv[me] = send[me]
+    gz[my_plane] = gsend[my_plane]
+    wait_bytes(gz, PLANES - 1, grecv_sem.at[0])
+
+    def spread(o, c):
+        in_plane_copy(o, gz, grecv, gsend_sem.at[1], grecv_sem.at[1]).start()
+        return c
+
+    lax.fori_loop(1, plane, spread, 0)
+    grecv[my_in] = gz[...]
     send_part(1, half_n, plane, False)
-    recv[me] = send[me]
-    grecv[me] = gsend[my_plane]
-    wait_bytes(send, plane, fsend_sem.at[0])
     send_part(2, 0, half_n, True)
-    wait_bytes(send, plane, fsend_sem.at[1])
     send_part(3, half_n, plane, False)
 
     def wait_chunk(ci, buf, sem):
@@ -155,29 +177,38 @@
         wcopies[i].wait()
     for i in (3, 4, 5):
         loads[i].wait()
+    wait_bytes(grecv, plane - 1, grecv_sem.at[1])
 
     lane_c = lax.broadcasted_iota(jnp.int32, (plane, cap, lanes), 2)
     sub_c = lax.broadcasted_iota(jnp.int32, (plane, cap, lanes), 1)
     mine = lane_c == my_in * cap + sub_c
 
     def plane_at(ci):
-        n = lax.rem(ci + 1, PLANES)
+        n = lax.rem(ci + 1, PLANES) if opt['order'] == 'near' else PLANES - 1 - ci
         dz = n + (n // 2) * (5 - 2 * n)
         return lax.rem(my_plane + dz, PLANES)
 
     def chunk(ci, c):
         zp = plane_at(ci)
         wait_chunk(ci, recv, frecv_sem.at[zp])
-        wait_chunk(ci, grecv, grecv_sem.at[zp])
         rows = pl.ds(zp * rows_chunk, rows_chunk)
         blocks = pl.ds(zp * plane, plane)
         dy = recv[blocks].astype(F32).reshape(rows_chunk, width)
-        gate3 = jnp.where(mine, jnp.broadcast_to(grecv[blocks], (plane, cap, lanes)), 0.0)
+        gate3 = jnp.where(mine, jnp.broadcast_to(grecv[:, zp], (plane, cap, lanes)), 0.0)
         gate = jnp.sum(gate3, axis=2, keepdims=True).reshape(rows_chunk, 1)
         g = (dy * gate).astype(BF16)
         gv[rows] = g
         val = jnp.sum(dy * yv[rows].astype(F32), axis=1, keepdims=True).reshape(plane, cap, 1)
-        vs[blocks] = jnp.sum(jnp.where(mine, val, 0.0), axis=1, keepdims=True)
+        vs[:, zp] = jnp.sum(jnp.where(mine, val, 0.0), axis=1, keepdims=True)
+
+        @pl.when(ci == PLANES - 1)
+        def _():
+            def gather_back(o, cc):
+                in_plane_copy(o, vs, vr, vsend_sem.at[0], vrecv_sem.at[0]).start()
+                return cc
+
+            lax.fori_loop(1, plane, gather_back, 0)
+
         da = lax.dot_general(g, wd[...], NT, preferred_element_type=F32)
         h1 = hgv[rows].astype(F32)
         h3 = huv[rows].astype(F32)
@@ -195,7 +226,6 @@
             @pl.when(jnp.logical_or(ci < PLANES - 1, o > 0))
             def _():
                 row_copy(dxs, dxr, idx, bsend_sem, brecv_sem).start()
-                row_copy(vs, vr, idx, vsend_sem, vrecv_sem).start()
 
             return cc
 
@@ -204,7 +234,7 @@
 
     lax.fori_loop(0, PLANES, chunk, 0)
     dxr[me] = dxs[me]
-    vr[me] = vs[me]
+    vr[my_in] = vs[my_in]
 
     loads[6].wait()
 
@@ -232,22 +262,28 @@
     pcopies.append(partner_copy(pd, rd, 2, psend_sem, precv_sem))
     pcopies[2].start()
     in_grads(q * half_d, og, ou)
+    wait_bytes(vr, plane - 1, vrecv_sem.at[0])
+    total = jnp.sum(vr[...], axis=0)
+    vsum[...] = total
+    back4[my_plane] = vsum[my_plane]
     out_grads(q * half_f, od)
+    for dz in range(1, PLANES):
+        line_copy(dz, vsum, back4, vsend_sem.at[1], vrecv_sem.at[1]).start()
     for i, (mine_ref, got) in enumerate(((og, rg), (ou, ru), (od, rd))):
         pcopies[i].wait()
         mine_ref[...] += got[...]
 
+    wait_bytes(back4, PLANES - 1, vrecv_sem.at[1])
     acc = jnp.zeros((tok_n, width), F32)
     vals = [jnp.zeros((lanes, tok_n), F32) for _ in range(top)]
     for ci, dz in enumerate(PLANE_ORDER):
         zp = lax.rem(my_plane + PLANES - dz, PLANES)
         n = plane - 1 if dz == 0 else plane
         wait_bytes(dxr, n, brecv_sem.at[zp])
-        wait_bytes(vr, n, vrecv_sem.at[zp])
         blocks = pl.ds(zp * plane, plane)
         part = dxr[blocks].astype(F32).reshape(rows_chunk, width).astype(BF16)
         acc = acc + lax.dot_general(onehot[zp], part, TN, preferred_element_type=F32)
-        back = jnp.sum(jnp.where(diag, jnp.sum(vr[blocks], axis=0), 0.0), axis=1, keepdims=True)
+        back = jnp.sum(jnp.where(diag, back4[zp], 0.0), axis=1, keepdims=True)
         for j in range(top):
             hit = slot_s == dest[j:j + 1, :] - zp * lanes
             vals[j] = jnp.where(hit, back, vals[j])
@@ -257,9 +293,13 @@
 
     wait_bytes(send, plane - 1, fsend_sem.at[2])
     wait_bytes(send, plane, fsend_sem.at[3])
-    wait_bytes(grecv, ep_n - 1, gsend_sem)
+    wait_bytes(send, plane, fsend_sem.at[0])
+    wait_bytes(send, plane, fsend_sem.at[1])
+    wait_bytes(gz, PLANES - 1, gsend_sem.at[0])
+    wait_bytes(grecv, plane - 1, gsend_sem.at[1])
     wait_bytes(dxs, ep_n - 1, bsend_sem)
-    wait_bytes(vs, ep_n - 1, vsend_sem)
+    wait_bytes(vr, plane - 1, vsend_sem.at[0])
+    wait_bytes(back4, PLANES - 1, vsend_sem.at[1])
 
 
 def write_kernel(*refs):
@@ -292,7 +332,8 @@
         hbm = pl.BlockSpec(memory_space=pltpu.HBM)
         dma = pltpu.SemaphoreType.DMA
         rows_buf = pltpu.VMEM((ep_n, cap, width), BF16)
-        gate_buf = pltpu.VMEM((ep_n, 1, lanes), F32)
+        line_buf = pltpu.VMEM((PLANES, 1, lanes), F32)
+        gate_buf = pltpu.VMEM((plane, PLANES, 1, lanes), F32)
         in_part = pltpu.VMEM((half_d, hidden), F32)
         out_part = pltpu.VMEM((half_f, width), F32)
         results = [
@@ -303,21 +344,21 @@
             jax.ShapeDtypeStruct((half_d, hidden), F32),
         ]
         outs = pl.pallas_call(
-            functools.partial(layer_kernel, cfg),
+            functools.partial(layer_kernel, cfg, OPT),
             out_shape=results,
             in_specs=[hbm] * 11,
             out_specs=[vmem] * 5,
             scratch_shapes=[
                 pltpu.VMEM((tok_n, width), BF16), pltpu.VMEM((top, tok_n), jnp.int32), pltpu.VMEM((top, tok_n), jnp.int32),
-                pltpu.VMEM((top, tok_n), F32), rows_buf, rows_buf, pltpu.VMEM((PLANES, 1, lanes), F32), gate_buf, rows_buf, rows_buf, gate_buf, gate_buf,
+                pltpu.VMEM((top, tok_n), F32), rows_buf, rows_buf, line_buf, line_buf, gate_buf, rows_buf, rows_buf, gate_buf, gate_buf, line_buf, line_buf,
                 pltpu.VMEM((rows, width), BF16), pltpu.VMEM((rows, width), BF16),
                 pltpu.VMEM((rows, hidden), BF16), pltpu.VMEM((rows, hidden), BF16),
                 pltpu.VMEM((width, 2 * hidden), BF16), pltpu.VMEM((hidden, width), BF16),
                 pltpu.VMEM((PLANES, lanes, tok_n), BF16),
                 pltpu.VMEM((rows, width), BF16), pltpu.VMEM((rows, hidden), BF16), pltpu.VMEM((rows, 2 * hidden), BF16),
                 in_part, out_part, in_part, in_part, out_part, in_part,
-                dma((11,)), dma((3,)), dma((3,)), dma((4,)), dma((PLANES,)), dma, dma((PLANES,)),
-                dma, dma((PLANES,)), dma, dma((PLANES,)), dma((3,)), dma((3,)),
+                dma((11,)), dma((3,)), dma((3,)), dma((4,)), dma((PLANES,)), dma((2,)), dma((2,)),
+                dma, dma((PLANES,)), dma((2,)), dma((2,)), dma((3,)), dma((3,)),
             ],
             compiler_params=pltpu.CompilerParams(collective_id=0, has_side_effects=True, vmem_limit_bytes=44 * 1024 * 1024),
             name='layer',

time: 67 us -> 65.6 us (0.979)
  the two profiles are of different devices: /device:TPU:49 before, /device:TPU:55 now
where the time goes in v5:
time: 65.6 us; the launch traced here: 65.4 us
  Pallas kernels  64.8 us (99%)
    pallas_call x1, Pallas kernels, local_backward(): pl.pallas_call(functools.partial(layer_kernel, cfg, OPT), out_shape=resul...  62.5 us
    pallas_call x1, Pallas kernels, local_backward(): pl.pallas_call(write_kernel, out_shape=results, in_specs=[vmem] * 5, out_...  2.29 us

profile of v5, /device:TPU:55, one launch (start us, length us, event | category | flops | bytes accessed | tf_op | source)
XLA Modules:
  0.0 65.4 jit_solution(893137744051549001)
XLA Ops:
  0.6 62.5 %layer.1 = (bf16[64,1536]{1,0:T(8,128)(2,1)S(1)}, f32[6,64]{1,0:T(8,128)S(1)}, f32[768,512]{1,0:T(8,128)S(1)}, f32[256,1536]{1,0:T(8,128)S(1)}, f32[768,512]{1,0:T(8,128)S(1)}) custom-call(bf16[64,1536]{1,0:T(8,128)(2,1)} %go_in.1, s32[6,64]{1,0:T(8,128)} %bitcast.21, s32[6,64]{1,0:T(8,128)} %bitcast.22, f32[6,64]{1,0:T(8,128)} %bitcast.23, ...), custom_call_target="tpu_custom_call" | custom-call | tf_op jit(solution)/shard_map/layer/pallas_call | solution.py:346
  63.1 2.3 %write.1 = (bf16[64,1536]{1,0:T(8,128)(2,1)}, f32[6,64]{1,0:T(8,128)}, f32[768,512]{1,0:T(8,128)}, f32[256,1536]{1,0:T(8,128)}, f32[768,512]{1,0:T(8,128)}) custom-call(bf16[64,1536]{1,0:T(8,128)(2,1)S(1)} %get-tuple-element.15.refs_0_, f32[6,64]{1,0:T(8,128)S(1)} %get-tuple-element.16.refs_1_, f32[768,512]{1,0:T(8,128)S(1)} %get-tuple-element.17.refs_2_, ...), custom_call_target="tpu_custom_call" | custom-call | tf_op jit(solution)/shard_map/write/pallas_call | solution.py:366

commit v6 on v5

--- a/solution.py
+++ b/solution.py
@@ -11,15 +11,11 @@
 F32 = jnp.float32
 BF16 = jnp.bfloat16
 PLANES = 4
-ORDERS = {'near': (1, 3, 2, 0), 'far': (2, 3, 1, 0)}
 NT = (((1,), (1,)), ((), ()))
 TN = (((0,), (0,)), ((), ()))
 
 
-OPT = dict(order='near', mirror=False)
-
-
-def layer_kernel(cfg, opt, go_in, eidx_in, slot_in, gates_in, x_in, hg_in, hu_in, y_in, wg_in, wd_in, wu_in,
+def layer_kernel(cfg, go_in, eidx_in, slot_in, gates_in, x_in, hg_in, hu_in, y_in, wg_in, wd_in, wu_in,
                  gx, gg, og, od, ou,
                  go, eidx, slot, gates, send, recv, gsend, gz, grecv, dxs, dxr, vs, vr, vsum, back4,
                  xv, yv, hgv, huv, wgu, wd, onehot, gv, av, dhv,
@@ -27,7 +23,6 @@
                  load_sem, wsend_sem, wrecv_sem, fsend_sem, frecv_sem, gsend_sem, grecv_sem,
                  bsend_sem, brecv_sem, vsend_sem, vrecv_sem, psend_sem, precv_sem):
     ep_n, top, tok_n, width, hidden, cap, ysz, xsz = cfg
-    PLANE_ORDER = ORDERS[opt['order']]
     plane = ep_n // PLANES
     lanes = plane * cap
     rows_chunk = plane * cap
@@ -38,15 +33,18 @@
     my_plane = me // plane
     my_in = lax.rem(me, plane)
 
+    my_y, my_x = my_in // xsz, lax.rem(my_in, xsz)
+
+    def walk(c, k, n):
+        return lax.rem(c + (1 - 2 * lax.rem(c, 2)) * k + n, n)
+
     def peer_in(o):
-        half, i = o // (plane // 2), lax.rem(o, plane // 2)
-        oy = i // (xsz // 2)
-        ox = 2 * lax.rem(i, xsz // 2) + lax.rem(oy + half, 2)
-        my_y, my_x = my_in // xsz, lax.rem(my_in, xsz)
-        if opt['mirror']:
-            oy = oy + lax.rem(my_y, 2) * (ysz - 2 * oy)
-            ox = ox + lax.rem(my_x, 2) * (xsz - 2 * ox)
-        return lax.rem(my_y + oy, ysz) * xsz + lax.rem(my_x + ox, xsz)
+        return walk(my_y, o // xsz, ysz) * xsz + walk(my_x, lax.rem(o, xsz), xsz)
+
+    def peer(pos):
+        o = lax.rem(pos, plane)
+        dz = lax.rem(o // xsz + lax.rem(o, xsz) + pos // plane, PLANES)
+        return walk(my_plane, dz, PLANES), peer_in(o)
 
     barrier = pltpu.get_barrier_semaphore()
 
@@ -67,26 +65,32 @@
         pltpu.make_async_copy(wd_in, wd.at[pl.ds(q * half_f, half_f)], load_sem.at[0]),
         pltpu.make_async_copy(wg_in, wgu.at[pl.ds(q * half_d, half_d), pl.ds(0, hidden)], load_sem.at[1]),
         pltpu.make_async_copy(wu_in, wgu.at[pl.ds(q * half_d, half_d), pl.ds(hidden, hidden)], load_sem.at[2]),
-        pltpu.make_async_copy(hg_in, hgv, load_sem.at[3]),
-        pltpu.make_async_copy(hu_in, huv, load_sem.at[4]),
-        pltpu.make_async_copy(y_in, yv, load_sem.at[5]),
-        pltpu.make_async_copy(x_in, xv, load_sem.at[6]),
     ]
     for cp in loads:
         cp.start()
 
     for cp in small:
         cp.wait()
-    dest = jnp.where(slot[...] >= 0, eidx[...] * cap + slot[...], ep_n * cap)
+    kept = slot[...] >= 0
+    dest = jnp.where(kept, eidx[...] * cap + slot[...], ep_n * cap)
+
+    def steps(place, c, n):
+        return ((1 - 2 * lax.rem(c, 2)) * (place - c) + 2 * n) & (n - 1)
+
+    place_in = eidx[...] & (plane - 1)
+    dz = steps(eidx[...] >> (plane.bit_length() - 1), my_plane, PLANES)
+    dy = steps(place_in >> (xsz.bit_length() - 1), my_y, ysz)
+    dx = steps(place_in & (xsz - 1), my_x, xsz)
+    pos_of = ((dz - dy - dx + 2 * PLANES) & (PLANES - 1)) * plane + dy * xsz + dx
+    dest_pos = jnp.where(kept, pos_of * cap + slot[...], ep_n * cap)
     slot_s = lax.broadcasted_iota(jnp.int32, (lanes, tok_n), 0)
     diag = lax.broadcasted_iota(jnp.int32, (lanes, lanes), 0) == lax.broadcasted_iota(jnp.int32, (lanes, lanes), 1)
     for k in range(PLANES):
         hot = jnp.zeros((lanes, tok_n), F32)
         gate = jnp.zeros((lanes, tok_n), F32)
         for j in range(top):
-            hit = slot_s == dest[j:j + 1, :] - k * lanes
-            hot = jnp.where(hit, 1.0, hot)
-            gate = jnp.where(hit, gates[j:j + 1, :], gate)
+            hot = jnp.where(slot_s == dest_pos[j:j + 1, :] - k * lanes, 1.0, hot)
+            gate = jnp.where(slot_s == dest[j:j + 1, :] - k * lanes, gates[j:j + 1, :], gate)
         hot = hot.astype(BF16)
         onehot[k] = hot
         gate_col = jnp.sum(gate, axis=1, keepdims=True)
@@ -108,9 +112,10 @@
     for cp in wcopies:
         cp.start()
 
-    def row_copy(src, dst, idx, ssem, rsem):
-        return pltpu.make_async_remote_copy(src_ref=src.at[idx], dst_ref=dst.at[me], send_sem=ssem,
-                                            recv_sem=rsem.at[my_plane], device_id=(q, idx), device_id_type=MESH)
+    def row_copy(src, dst, pos, ssem, rsem):
+        zt, it = peer(pos)
+        return pltpu.make_async_remote_copy(src_ref=src.at[pos], dst_ref=dst.at[pos], send_sem=ssem,
+                                            recv_sem=rsem.at[pos // plane], device_id=(q, zt * plane + it), device_id_type=MESH)
 
     def line_copy(dz, src, dst, ssem, rsem):
         zt = lax.rem(my_plane + dz, PLANES)
@@ -127,29 +132,17 @@
         part = buf.at[pl.ds(0, n)]
         pltpu.make_async_copy(part, part, sem).wait()
 
-    def send_part(part, lo, hi, skip_own):
-        first, second = PLANE_ORDER[2 * (part // 2)], PLANE_ORDER[2 * (part // 2) + 1]
-
-        def send_one(o, c):
-            for dz in (first, second):
-                idx = lax.rem(my_plane + PLANES - dz, PLANES) * plane + peer_in(o)
-
-                def go_now():
-                    row_copy(send, recv, idx, fsend_sem.at[part], frecv_sem).start()
-
-                if dz == 0 and skip_own:
-                    pl.when(o > 0)(go_now)
-                else:
-                    go_now()
+    def send_rows(lo, hi):
+        def send_one(pos, c):
+            row_copy(send, recv, pos, fsend_sem, frecv_sem).start()
             return c
 
         lax.fori_loop(lo, hi, send_one, 0)
 
-    half_n = plane // 2
     for dz in range(1, PLANES):
         line_copy(dz, gsend, gz, gsend_sem.at[0], grecv_sem.at[0]).start()
-    send_part(0, 0, half_n, False)
-    recv[me] = send[me]
+    send_rows(1, plane)
+    recv[0] = send[0]
     gz[my_plane] = gsend[my_plane]
     wait_bytes(gz, PLANES - 1, grecv_sem.at[0])
 
@@ -159,47 +152,54 @@
 
     lax.fori_loop(1, plane, spread, 0)
     grecv[my_in] = gz[...]
-    send_part(1, half_n, plane, False)
-    send_part(2, 0, half_n, True)
-    send_part(3, half_n, plane, False)
+    send_rows(plane, ep_n)
+
+    def load_block(pos, c):
+        zt, it = peer(pos)
+        src = zt * plane + it
+        pltpu.make_async_copy(hg_in.at[src], hgv.at[pos], load_sem.at[3]).start()
+        pltpu.make_async_copy(hu_in.at[src], huv.at[pos], load_sem.at[4]).start()
+        pltpu.make_async_copy(y_in.at[src], yv.at[pos], load_sem.at[5]).start()
+        pltpu.make_async_copy(x_in.at[src], xv.at[pos], load_sem.at[6]).start()
+        return c
+
+    lax.fori_loop(0, ep_n, load_block, 0)
 
     def wait_chunk(ci, buf, sem):
-        @pl.when(ci < PLANES - 1)
+        @pl.when(ci > 0)
         def _():
             wait_bytes(buf, plane, sem)
 
-        @pl.when(ci == PLANES - 1)
+        @pl.when(ci == 0)
         def _():
             wait_bytes(buf, plane - 1, sem)
 
     for i in (0, 1, 2):
         loads[i].wait()
         wcopies[i].wait()
-    for i in (3, 4, 5):
-        loads[i].wait()
+    wait_bytes(hgv, ep_n, load_sem.at[3])
+    wait_bytes(huv, ep_n, load_sem.at[4])
+    wait_bytes(yv, ep_n, load_sem.at[5])
     wait_bytes(grecv, plane - 1, grecv_sem.at[1])
 
     lane_c = lax.broadcasted_iota(jnp.int32, (plane, cap, lanes), 2)
     sub_c = lax.broadcasted_iota(jnp.int32, (plane, cap, lanes), 1)
     mine = lane_c == my_in * cap + sub_c
 
-    def plane_at(ci):
-        n = lax.rem(ci + 1, PLANES) if opt['order'] == 'near' else PLANES - 1 - ci
-        dz = n + (n // 2) * (5 - 2 * n)
-        return lax.rem(my_plane + dz, PLANES)
-
     def chunk(ci, c):
-        zp = plane_at(ci)
-        wait_chunk(ci, recv, frecv_sem.at[zp])
-        rows = pl.ds(zp * rows_chunk, rows_chunk)
-        blocks = pl.ds(zp * plane, plane)
+        wait_chunk(ci, recv, frecv_sem.at[ci])
+        rows = pl.ds(ci * rows_chunk, rows_chunk)
+        blocks = pl.ds(ci * plane, plane)
+        places = [peer(ci * plane + i) for i in range(plane)]
         dy = recv[blocks].astype(F32).reshape(rows_chunk, width)
-        gate3 = jnp.where(mine, jnp.broadcast_to(grecv[:, zp], (plane, cap, lanes)), 0.0)
+        gate3 = jnp.where(mine, jnp.broadcast_to(jnp.stack([grecv[it, zt] for zt, it in places]), (plane, cap, lanes)), 0.0)
         gate = jnp.sum(gate3, axis=2, keepdims=True).reshape(rows_chunk, 1)
         g = (dy * gate).astype(BF16)
         gv[rows] = g
-        val = jnp.sum(dy * yv[rows].astype(F32), axis=1, keepdims=True).reshape(plane, cap, 1)
-        vs[:, zp] = jnp.sum(jnp.where(mine, val, 0.0), axis=1, keepdims=True)
+        val = jnp.sum(dy * yv[blocks].astype(F32).reshape(rows_chunk, width), axis=1, keepdims=True).reshape(plane, cap, 1)
+        spread_val = jnp.sum(jnp.where(mine, val, 0.0), axis=1, keepdims=True)
+        for i, (zt, it) in enumerate(places):
+            vs[it, zt] = spread_val[i]
 
         @pl.when(ci == PLANES - 1)
         def _():
@@ -210,8 +210,8 @@
             lax.fori_loop(1, plane, gather_back, 0)
 
         da = lax.dot_general(g, wd[...], NT, preferred_element_type=F32)
-        h1 = hgv[rows].astype(F32)
-        h3 = huv[rows].astype(F32)
+        h1 = hgv[blocks].astype(F32).reshape(rows_chunk, hidden)
+        h3 = huv[blocks].astype(F32).reshape(rows_chunk, hidden)
         sg = jax.nn.sigmoid(h1)
         silu = h1 * sg
         av[rows] = jnp.where(gate > 0.0, silu * h3, 0.0).astype(BF16)
@@ -221,11 +221,11 @@
         dxs[blocks] = dx.reshape(plane, cap, width).astype(BF16)
 
         def back_one(o, cc):
-            idx = zp * plane + peer_in(o)
-
-            @pl.when(jnp.logical_or(ci < PLANES - 1, o > 0))
+            pos = ci * plane + o
+
+            @pl.when(pos > 0)
             def _():
-                row_copy(dxs, dxr, idx, bsend_sem, brecv_sem).start()
+                row_copy(dxs, dxr, pos, bsend_sem, brecv_sem).start()
 
             return cc
 
@@ -233,17 +233,18 @@
         return c
 
     lax.fori_loop(0, PLANES, chunk, 0)
-    dxr[me] = dxs[me]
+    dxr[0] = dxs[0]
     vr[my_in] = vs[my_in]
 
-    loads[6].wait()
+    wait_bytes(xv, ep_n, load_sem.at[6])
 
     def in_grads(base, to_g, to_u):
         tile = 256 if half_d % 256 == 0 else half_d
 
         def step(i, c):
             cols = pl.ds(pl.multiple_of(base + i * tile, tile), tile)
-            r = lax.dot_general(xv[:, cols], dhv[...], TN, preferred_element_type=F32)
+            xt = xv[:, :, cols].astype(F32).reshape(ep_n * cap, tile).astype(BF16)
+            r = lax.dot_general(xt, dhv[...], TN, preferred_element_type=F32)
             to_g[pl.ds(i * tile, tile)] = r[:, :hidden]
             to_u[pl.ds(i * tile, tile)] = r[:, hidden:]
             return c
@@ -276,10 +277,8 @@
     wait_bytes(back4, PLANES - 1, vrecv_sem.at[1])
     acc = jnp.zeros((tok_n, width), F32)
     vals = [jnp.zeros((lanes, tok_n), F32) for _ in range(top)]
-    for ci, dz in enumerate(PLANE_ORDER):
-        zp = lax.rem(my_plane + PLANES - dz, PLANES)
-        n = plane - 1 if dz == 0 else plane
-        wait_bytes(dxr, n, brecv_sem.at[zp])
+    for zp in range(PLANES):
+        wait_bytes(dxr, plane - 1 if zp == 0 else plane, brecv_sem.at[zp])
         blocks = pl.ds(zp * plane, plane)
         part = dxr[blocks].astype(F32).reshape(rows_chunk, width).astype(BF16)
         acc = acc + lax.dot_general(onehot[zp], part, TN, preferred_element_type=F32)
@@ -291,10 +290,7 @@
     for j in range(top):
         gg[j:j + 1, :] = jnp.sum(vals[j], axis=0, keepdims=True)
 
-    wait_bytes(send, plane - 1, fsend_sem.at[2])
-    wait_bytes(send, plane, fsend_sem.at[3])
-    wait_bytes(send, plane, fsend_sem.at[0])
-    wait_bytes(send, plane, fsend_sem.at[1])
+    wait_bytes(send, ep_n - 1, fsend_sem)
     wait_bytes(gz, PLANES - 1, gsend_sem.at[0])
     wait_bytes(grecv, plane - 1, gsend_sem.at[1])
     wait_bytes(dxs, ep_n - 1, bsend_sem)
@@ -344,25 +340,24 @@
             jax.ShapeDtypeStruct((half_d, hidden), F32),
         ]
         outs = pl.pallas_call(
-            functools.partial(layer_kernel, cfg, OPT),
+            functools.partial(layer_kernel, cfg),
             out_shape=results,
             in_specs=[hbm] * 11,
             out_specs=[vmem] * 5,
             scratch_shapes=[
                 pltpu.VMEM((tok_n, width), BF16), pltpu.VMEM((top, tok_n), jnp.int32), pltpu.VMEM((top, tok_n), jnp.int32),
                 pltpu.VMEM((top, tok_n), F32), rows_buf, rows_buf, line_buf, line_buf, gate_buf, rows_buf, rows_buf, gate_buf, gate_buf, line_buf, line_buf,
-                pltpu.VMEM((rows, width), BF16), pltpu.VMEM((rows, width), BF16),
-                pltpu.VMEM((rows, hidden), BF16), pltpu.VMEM((rows, hidden), BF16),
+                rows_buf, rows_buf, pltpu.VMEM((ep_n, cap, hidden), BF16), pltpu.VMEM((ep_n, cap, hidden), BF16),
                 pltpu.VMEM((width, 2 * hidden), BF16), pltpu.VMEM((hidden, width), BF16),
                 pltpu.VMEM((PLANES, lanes, tok_n), BF16),
                 pltpu.VMEM((rows, width), BF16), pltpu.VMEM((rows, hidden), BF16), pltpu.VMEM((rows, 2 * hidden), BF16),
                 in_part, out_part, in_part, in_part, out_part, in_part,
-                dma((11,)), dma((3,)), dma((3,)), dma((4,)), dma((PLANES,)), dma((2,)), dma((2,)),
+                dma((11,)), dma((3,)), dma((3,)), dma, dma((PLANES,)), dma((2,)), dma((2,)),
                 dma, dma((PLANES,)), dma((2,)), dma((2,)), dma((3,)), dma((3,)),
             ],
             compiler_params=pltpu.CompilerParams(collective_id=0, has_side_effects=True, vmem_limit_bytes=44 * 1024 * 1024),
             name='layer',
-        )(*[pltpu.with_memory_space_constraint(v, pltpu.HBM) for v in (grad_out, expert_idx.T, slot_pos.T, gates.T, x_disp[0], h_gate[0], h_up[0], y_disp[0], w_gate[0], w_down[0], w_up[0])])
+        )(*[pltpu.with_memory_space_constraint(v, pltpu.HBM) for v in (grad_out, expert_idx.T, slot_pos.T, gates.T, *[v.reshape(ep_n, cap, v.shape[2]) for v in (x_disp, h_gate, h_up, y_disp)], w_gate[0], w_down[0], w_up[0])])
         gx, gg, dwg, dwd, dwu = pl.pallas_call(
             write_kernel,
             out_shape=results,

time: 65.6 us -> 60.2 us (0.918)
  the two profiles are of different devices: /device:TPU:55 before, /device:TPU:0 now
where the time goes in v6:
time: 60.2 us; the launch traced here: 60 us
  Pallas kernels  59.4 us (99%)
  between operations  0.64 us (1%)
    pallas_call x1, Pallas kernels, local_backward(): pl.pallas_call(functools.partial(layer_kernel, cfg), out_shape=results, i...  57.1 us
    pallas_call x1, Pallas kernels, local_backward(): pl.pallas_call(write_kernel, out_shape=results, in_specs=[vmem] * 5, out_...  2.29 us

profile of v6, /device:TPU:0, one launch (start us, length us, event | category | flops | bytes accessed | tf_op | source)
XLA Modules:
  0.0 60.0 jit_solution(7732021043230963696)
XLA Ops:
  0.6 57.1 %layer.1 = (bf16[64,1536]{1,0:T(8,128)(2,1)S(1)}, f32[6,64]{1,0:T(8,128)S(1)}, f32[768,512]{1,0:T(8,128)S(1)}, f32[256,1536]{1,0:T(8,128)S(1)}, f32[768,512]{1,0:T(8,128)S(1)}) custom-call(bf16[64,1536]{1,0:T(8,128)(2,1)} %go_in.1, s32[6,64]{1,0:T(8,128)} %bitcast.21, s32[6,64]{1,0:T(8,128)} %bitcast.22, f32[6,64]{1,0:T(8,128)} %bitcast.23, ...), custom_call_target="tpu_custom_call" | custom-call | tf_op jit(solution)/shard_map/layer/pallas_call | solution.py:342
  57.7 2.3 %write.1 = (bf16[64,1536]{1,0:T(8,128)(2,1)}, f32[6,64]{1,0:T(8,128)}, f32[768,512]{1,0:T(8,128)}, f32[256,1536]{1,0:T(8,128)}, f32[768,512]{1,0:T(8,128)}) custom-call(bf16[64,1536]{1,0:T(8,128)(2,1)S(1)} %get-tuple-element.15.refs_0_, f32[6,64]{1,0:T(8,128)S(1)} %get-tuple-element.16.refs_1_, f32[768,512]{1,0:T(8,128)S(1)} %get-tuple-element.17.refs_2_, ...), custom_call_target="tpu_custom_call" | custom-call | tf_op jit(solution)/shard_map/write/pallas_call | solution.py:361

commit v7 on v6

--- a/solution.py
+++ b/solution.py
@@ -98,62 +98,6 @@
         picked = jnp.dot(hot, go[...], preferred_element_type=F32)
         send[pl.ds(k * plane, plane)] = picked.reshape(plane, cap, width).astype(BF16)
 
-    pl.semaphore_wait(barrier, ep_n)
-
-    def partner_copy(src, dst, i, ssem, rsem):
-        return pltpu.make_async_remote_copy(src_ref=src, dst_ref=dst, send_sem=ssem.at[i], recv_sem=rsem.at[i],
-                                            device_id=(other, me), device_id_type=MESH)
-
-    wcopies = [
-        partner_copy(wd_in, wd.at[pl.ds(q * half_f, half_f)], 0, wsend_sem, wrecv_sem),
-        partner_copy(wg_in, wgu.at[pl.ds(q * half_d, half_d), pl.ds(0, hidden)], 1, wsend_sem, wrecv_sem),
-        partner_copy(wu_in, wgu.at[pl.ds(q * half_d, half_d), pl.ds(hidden, hidden)], 2, wsend_sem, wrecv_sem),
-    ]
-    for cp in wcopies:
-        cp.start()
-
-    def row_copy(src, dst, pos, ssem, rsem):
-        zt, it = peer(pos)
-        return pltpu.make_async_remote_copy(src_ref=src.at[pos], dst_ref=dst.at[pos], send_sem=ssem,
-                                            recv_sem=rsem.at[pos // plane], device_id=(q, zt * plane + it), device_id_type=MESH)
-
-    def line_copy(dz, src, dst, ssem, rsem):
-        zt = lax.rem(my_plane + dz, PLANES)
-        return pltpu.make_async_remote_copy(src_ref=src.at[zt], dst_ref=dst.at[my_plane], send_sem=ssem, recv_sem=rsem,
-                                            device_id=(q, zt * plane + my_in), device_id_type=MESH)
-
-    def in_plane_copy(o, src, dst, ssem, rsem):
-        to = peer_in(o)
-        part = src if len(src.shape) == 3 else src.at[to]
-        return pltpu.make_async_remote_copy(src_ref=part, dst_ref=dst.at[my_in], send_sem=ssem, recv_sem=rsem,
-                                            device_id=(q, my_plane * plane + to), device_id_type=MESH)
-
-    def wait_bytes(buf, n, sem):
-        part = buf.at[pl.ds(0, n)]
-        pltpu.make_async_copy(part, part, sem).wait()
-
-    def send_rows(lo, hi):
-        def send_one(pos, c):
-            row_copy(send, recv, pos, fsend_sem, frecv_sem).start()
-            return c
-
-        lax.fori_loop(lo, hi, send_one, 0)
-
-    for dz in range(1, PLANES):
-        line_copy(dz, gsend, gz, gsend_sem.at[0], grecv_sem.at[0]).start()
-    send_rows(1, plane)
-    recv[0] = send[0]
-    gz[my_plane] = gsend[my_plane]
-    wait_bytes(gz, PLANES - 1, grecv_sem.at[0])
-
-    def spread(o, c):
-        in_plane_copy(o, gz, grecv, gsend_sem.at[1], grecv_sem.at[1]).start()
-        return c
-
-    lax.fori_loop(1, plane, spread, 0)
-    grecv[my_in] = gz[...]
-    send_rows(plane, ep_n)
-
     def load_block(pos, c):
         zt, it = peer(pos)
         src = zt * plane + it
@@ -164,6 +108,64 @@
         return c
 
     lax.fori_loop(0, ep_n, load_block, 0)
+
+    pl.semaphore_wait(barrier, ep_n)
+
+    def partner_copy(src, dst, i, ssem, rsem):
+        return pltpu.make_async_remote_copy(src_ref=src, dst_ref=dst, send_sem=ssem.at[i], recv_sem=rsem.at[i],
+                                            device_id=(other, me), device_id_type=MESH)
+
+    wcopies = [
+        partner_copy(wd_in, wd.at[pl.ds(q * half_f, half_f)], 0, wsend_sem, wrecv_sem),
+        partner_copy(wg_in, wgu.at[pl.ds(q * half_d, half_d), pl.ds(0, hidden)], 1, wsend_sem, wrecv_sem),
+        partner_copy(wu_in, wgu.at[pl.ds(q * half_d, half_d), pl.ds(hidden, hidden)], 2, wsend_sem, wrecv_sem),
+    ]
+
+    def row_copy(src, dst, pos, ssem, rsem):
+        zt, it = peer(pos)
+        return pltpu.make_async_remote_copy(src_ref=src.at[pos], dst_ref=dst.at[pos], send_sem=ssem,
+                                            recv_sem=rsem.at[pos // plane], device_id=(q, zt * plane + it), device_id_type=MESH)
+
+    def line_copy(dz, src, dst, ssem, rsem):
+        zt = lax.rem(my_plane + dz, PLANES)
+        return pltpu.make_async_remote_copy(src_ref=src.at[zt], dst_ref=dst.at[my_plane], send_sem=ssem, recv_sem=rsem,
+                                            device_id=(q, zt * plane + my_in), device_id_type=MESH)
+
+    def in_plane_copy(o, src, dst, ssem, rsem):
+        to = peer_in(o)
+        part = src if len(src.shape) == 3 else src.at[to]
+        return pltpu.make_async_remote_copy(src_ref=part, dst_ref=dst.at[my_in], send_sem=ssem, recv_sem=rsem,
+                                            device_id=(q, my_plane * plane + to), device_id_type=MESH)
+
+    def wait_bytes(buf, n, sem):
+        part = buf.at[pl.ds(0, n)]
+        pltpu.make_async_copy(part, part, sem).wait()
+
+    def send_rows(lo, hi):
+        def send_one(pos, c):
+            row_copy(send, recv, pos, fsend_sem, frecv_sem).start()
+            return c
+
+        lax.fori_loop(lo, hi, send_one, 0)
+
+    for dz in range(1, PLANES):
+        line_copy(dz, gsend, gz, gsend_sem.at[0], grecv_sem.at[0]).start()
+    send_rows(1, plane)
+    for cp in wcopies:
+        cp.start()
+    send_rows(plane, 2 * plane)
+    recv[0] = send[0]
+    gz[my_plane] = gsend[my_plane]
+    wait_bytes(gz, PLANES - 1, grecv_sem.at[0])
+
+    def spread(o, c):
+        in_plane_copy(o, gz, grecv, gsend_sem.at[1], grecv_sem.at[1]).start()
+        return c
+
+    lax.fori_loop(1, plane, spread, 0)
+    grecv[my_in] = gz[...]
+    send_rows(2 * plane, ep_n)
+
 
     def wait_chunk(ci, buf, sem):
         @pl.when(ci > 0)

time: 60.2 us -> 61.1 us (1.015)
  the two profiles are of different devices: /device:TPU:0 before, /device:TPU:2 now
where the time goes in v7:
time: 61.1 us; the launch traced here: 61 us
  Pallas kernels  60.3 us (99%)
  between operations  0.64 us (1%)
    pallas_call x1, Pallas kernels, local_backward(): pl.pallas_call(functools.partial(layer_kernel, cfg), out_shape=results, i...  58 us
    pallas_call x1, Pallas kernels, local_backward(): pl.pallas_call(write_kernel, out_shape=results, in_specs=[vmem] * 5, out_...  2.29 us

profile of v7, /device:TPU:2, one launch (start us, length us, event | category | flops | bytes accessed | tf_op | source)
XLA Modules:
  0.0 61.0 jit_solution(11860949917559210918)
XLA Ops:
  0.6 58.0 %layer.1 = (bf16[64,1536]{1,0:T(8,128)(2,1)S(1)}, f32[6,64]{1,0:T(8,128)S(1)}, f32[768,512]{1,0:T(8,128)S(1)}, f32[256,1536]{1,0:T(8,128)S(1)}, f32[768,512]{1,0:T(8,128)S(1)}) custom-call(bf16[64,1536]{1,0:T(8,128)(2,1)} %go_in.1, s32[6,64]{1,0:T(8,128)} %bitcast.21, s32[6,64]{1,0:T(8,128)} %bitcast.22, f32[6,64]{1,0:T(8,128)} %bitcast.23, ...), custom_call_target="tpu_custom_call" | custom-call | tf_op jit(solution)/shard_map/layer/pallas_call | solution.py:344
  58.7 2.3 %write.1 = (bf16[64,1536]{1,0:T(8,128)(2,1)}, f32[6,64]{1,0:T(8,128)}, f32[768,512]{1,0:T(8,128)}, f32[256,1536]{1,0:T(8,128)}, f32[768,512]{1,0:T(8,128)}) custom-call(bf16[64,1536]{1,0:T(8,128)(2,1)S(1)} %get-tuple-element.15.refs_0_, f32[6,64]{1,0:T(8,128)S(1)} %get-tuple-element.16.refs_1_, f32[768,512]{1,0:T(8,128)S(1)} %get-tuple-element.17.refs_2_, ...), custom_call_target="tpu_custom_call" | custom-call | tf_op jit(solution)/shard_map/write/pallas_call | solution.py:363

commit v8 on v6

--- a/solution.py
+++ b/solution.py
@@ -13,6 +13,33 @@
 PLANES = 4
 NT = (((1,), (1,)), ((), ()))
 TN = (((0,), (0,)), ((), ()))
+
+
+def far_first(ysz, xsz):
+    left = [(dz, dy, dx) for dz in range(PLANES) for dy in range(ysz) for dx in range(xsz)]
+    sizes = (PLANES, ysz, xsz)
+
+    def hops(o):
+        return sum(min(k, n - k) for k, n in zip(o, sizes))
+
+    load, order = [0] * 6, []
+
+    def added(o):
+        new = list(load)
+        for d, (k, n) in enumerate(zip(o, sizes)):
+            if 2 * k <= n:
+                new[2 * d] += k
+            if 2 * k >= n and k:
+                new[2 * d + 1] += n - k
+        return new
+
+    while left:
+        most = max(hops(o) for o in left)
+        best = min((o for o in left if hops(o) == most), key=lambda o: (max(added(o)), sum(v * v for v in added(o)), o))
+        load = added(best)
+        order.append(best)
+        left.remove(best)
+    return order
 
 
 def layer_kernel(cfg, go_in, eidx_in, slot_in, gates_in, x_in, hg_in, hu_in, y_in, wg_in, wd_in, wu_in,
@@ -41,10 +68,12 @@
     def peer_in(o):
         return walk(my_y, o // xsz, ysz) * xsz + walk(my_x, lax.rem(o, xsz), xsz)
 
+    offsets = far_first(ysz, xsz)
+    own = ep_n - 1
+
     def peer(pos):
-        o = lax.rem(pos, plane)
-        dz = lax.rem(o // xsz + lax.rem(o, xsz) + pos // plane, PLANES)
-        return walk(my_plane, dz, PLANES), peer_in(o)
+        dz, dy, dx = offsets[pos]
+        return walk(my_plane, dz, PLANES), walk(my_y, dy, ysz) * xsz + walk(my_x, dx, xsz)
 
     barrier = pltpu.get_barrier_semaphore()
 
@@ -81,7 +110,10 @@
     dz = steps(eidx[...] >> (plane.bit_length() - 1), my_plane, PLANES)
     dy = steps(place_in >> (xsz.bit_length() - 1), my_y, ysz)
     dx = steps(place_in & (xsz - 1), my_x, xsz)
-    pos_of = ((dz - dy - dx + 2 * PLANES) & (PLANES - 1)) * plane + dy * xsz + dx
+    off = (dz * ysz + dy) * xsz + dx
+    pos_of = jnp.zeros_like(off)
+    for pos, (kz, ky, kx) in enumerate(offsets):
+        pos_of = jnp.where(off == (kz * ysz + ky) * xsz + kx, pos, pos_of)
     dest_pos = jnp.where(kept, pos_of * cap + slot[...], ep_n * cap)
     slot_s = lax.broadcasted_iota(jnp.int32, (lanes, tok_n), 0)
     diag = lax.broadcasted_iota(jnp.int32, (lanes, lanes), 0) == lax.broadcasted_iota(jnp.int32, (lanes, lanes), 1)
@@ -133,16 +165,13 @@
         pltpu.make_async_copy(part, part, sem).wait()
 
     def send_rows(lo, hi):
-        def send_one(pos, c):
+        for pos in range(lo, hi):
             row_copy(send, recv, pos, fsend_sem, frecv_sem).start()
-            return c
-
-        lax.fori_loop(lo, hi, send_one, 0)
 
     for dz in range(1, PLANES):
         line_copy(dz, gsend, gz, gsend_sem.at[0], grecv_sem.at[0]).start()
-    send_rows(1, plane)
-    recv[0] = send[0]
+    send_rows(0, plane)
+    recv[own] = send[own]
     gz[my_plane] = gsend[my_plane]
     wait_bytes(gz, PLANES - 1, grecv_sem.at[0])
 
@@ -152,27 +181,18 @@
 
     lax.fori_loop(1, plane, spread, 0)
     grecv[my_in] = gz[...]
-    send_rows(plane, ep_n)
-
-    def load_block(pos, c):
+    send_rows(plane, own)
+
+    for pos in range(ep_n):
         zt, it = peer(pos)
         src = zt * plane + it
         pltpu.make_async_copy(hg_in.at[src], hgv.at[pos], load_sem.at[3]).start()
         pltpu.make_async_copy(hu_in.at[src], huv.at[pos], load_sem.at[4]).start()
         pltpu.make_async_copy(y_in.at[src], yv.at[pos], load_sem.at[5]).start()
         pltpu.make_async_copy(x_in.at[src], xv.at[pos], load_sem.at[6]).start()
-        return c
-
-    lax.fori_loop(0, ep_n, load_block, 0)
-
-    def wait_chunk(ci, buf, sem):
-        @pl.when(ci > 0)
-        def _():
-            wait_bytes(buf, plane, sem)
-
-        @pl.when(ci == 0)
-        def _():
-            wait_bytes(buf, plane - 1, sem)
+
+    def in_chunk(ci):
+        return plane - 1 if ci == PLANES - 1 else plane
 
     for i in (0, 1, 2):
         loads[i].wait()
@@ -186,8 +206,8 @@
     sub_c = lax.broadcasted_iota(jnp.int32, (plane, cap, lanes), 1)
     mine = lane_c == my_in * cap + sub_c
 
-    def chunk(ci, c):
-        wait_chunk(ci, recv, frecv_sem.at[ci])
+    def chunk(ci):
+        wait_bytes(recv, in_chunk(ci), frecv_sem.at[ci])
         rows = pl.ds(ci * rows_chunk, rows_chunk)
         blocks = pl.ds(ci * plane, plane)
         places = [peer(ci * plane + i) for i in range(plane)]
@@ -201,8 +221,7 @@
         for i, (zt, it) in enumerate(places):
             vs[it, zt] = spread_val[i]
 
-        @pl.when(ci == PLANES - 1)
-        def _():
+        if ci == PLANES - 1:
             def gather_back(o, cc):
                 in_plane_copy(o, vs, vr, vsend_sem.at[0], vrecv_sem.at[0]).start()
                 return cc
@@ -220,20 +239,12 @@
         dx = lax.dot_general(dhv[rows], wgu[...], NT, preferred_element_type=F32)
         dxs[blocks] = dx.reshape(plane, cap, width).astype(BF16)
 
-        def back_one(o, cc):
-            pos = ci * plane + o
-
-            @pl.when(pos > 0)
-            def _():
-                row_copy(dxs, dxr, pos, bsend_sem, brecv_sem).start()
-
-            return cc
-
-        lax.fori_loop(0, plane, back_one, 0)
-        return c
-
-    lax.fori_loop(0, PLANES, chunk, 0)
-    dxr[0] = dxs[0]
+        for i in range(in_chunk(ci)):
+            row_copy(dxs, dxr, ci * plane + i, bsend_sem, brecv_sem).start()
+
+    for ci in range(PLANES):
+        chunk(ci)
+    dxr[own] = dxs[own]
     vr[my_in] = vs[my_in]
 
     wait_bytes(xv, ep_n, load_sem.at[6])
@@ -278,7 +289,7 @@
     acc = jnp.zeros((tok_n, width), F32)
     vals = [jnp.zeros((lanes, tok_n), F32) for _ in range(top)]
     for zp in range(PLANES):
-        wait_bytes(dxr, plane - 1 if zp == 0 else plane, brecv_sem.at[zp])
+        wait_bytes(dxr, in_chunk(zp), brecv_sem.at[zp])
         blocks = pl.ds(zp * plane, plane)
         part = dxr[blocks].astype(F32).reshape(rows_chunk, width).astype(BF16)
         acc = acc + lax.dot_general(onehot[zp], part, TN, preferred_element_type=F32)

time: 60.2 us -> 66 us (1.096)
  the two profiles are of different devices: /device:TPU:0 before, /device:TPU:2 now
where the time goes in v8:
time: 66 us; the launch traced here: 65.8 us
  Pallas kernels  65.2 us (99%)
    pallas_call x1, Pallas kernels, local_backward(): pl.pallas_call(functools.partial(layer_kernel, cfg), out_shape=results, i...  62.9 us
    pallas_call x1, Pallas kernels, local_backward(): pl.pallas_call(write_kernel, out_shape=results, in_specs=[vmem] * 5, out_...  2.29 us

profile of v8, /device:TPU:2, one launch (start us, length us, event | category | flops | bytes accessed | tf_op | source)
XLA Modules:
  0.0 65.8 jit_solution(5647883812998206890)
XLA Ops:
  0.6 62.9 %layer.1 = (bf16[64,1536]{1,0:T(8,128)(2,1)S(1)}, f32[6,64]{1,0:T(8,128)S(1)}, f32[768,512]{1,0:T(8,128)S(1)}, f32[256,1536]{1,0:T(8,128)S(1)}, f32[768,512]{1,0:T(8,128)S(1)}) custom-call(bf16[64,1536]{1,0:T(8,128)(2,1)} %go_in.1, s32[6,64]{1,0:T(8,128)} %bitcast.21, s32[6,64]{1,0:T(8,128)} %bitcast.22, f32[6,64]{1,0:T(8,128)} %bitcast.23, ...), custom_call_target="tpu_custom_call" | custom-call | tf_op jit(solution)/shard_map/layer/pallas_call | solution.py:353
  63.5 2.3 %write.1 = (bf16[64,1536]{1,0:T(8,128)(2,1)}, f32[6,64]{1,0:T(8,128)}, f32[768,512]{1,0:T(8,128)}, f32[256,1536]{1,0:T(8,128)}, f32[768,512]{1,0:T(8,128)}) custom-call(bf16[64,1536]{1,0:T(8,128)(2,1)S(1)} %get-tuple-element.15.refs_0_, f32[6,64]{1,0:T(8,128)S(1)} %get-tuple-element.16.refs_1_, f32[768,512]{1,0:T(8,128)S(1)} %get-tuple-element.17.refs_2_, ...), custom_call_target="tpu_custom_call" | custom-call | tf_op jit(solution)/shard_map/write/pallas_call | solution.py:372

commit v9 on v8

--- a/solution.py
+++ b/solution.py
@@ -15,31 +15,9 @@
 TN = (((0,), (0,)), ((), ()))
 
 
-def far_first(ysz, xsz):
-    left = [(dz, dy, dx) for dz in range(PLANES) for dy in range(ysz) for dx in range(xsz)]
-    sizes = (PLANES, ysz, xsz)
-
-    def hops(o):
-        return sum(min(k, n - k) for k, n in zip(o, sizes))
-
-    load, order = [0] * 6, []
-
-    def added(o):
-        new = list(load)
-        for d, (k, n) in enumerate(zip(o, sizes)):
-            if 2 * k <= n:
-                new[2 * d] += k
-            if 2 * k >= n and k:
-                new[2 * d + 1] += n - k
-        return new
-
-    while left:
-        most = max(hops(o) for o in left)
-        best = min((o for o in left if hops(o) == most), key=lambda o: (max(added(o)), sum(v * v for v in added(o)), o))
-        load = added(best)
-        order.append(best)
-        left.remove(best)
-    return order
+def even_chunks(ysz, xsz):
+    order = [((dy + dx + k) % PLANES, dy, dx) for k in (1, 2, 3, 0) for dy in range(ysz) for dx in range(xsz)]
+    return [o for o in order if o != (0, 0, 0)] + [(0, 0, 0)]
 
 
 def layer_kernel(cfg, go_in, eidx_in, slot_in, gates_in, x_in, hg_in, hu_in, y_in, wg_in, wd_in, wu_in,
@@ -68,7 +46,7 @@
     def peer_in(o):
         return walk(my_y, o // xsz, ysz) * xsz + walk(my_x, lax.rem(o, xsz), xsz)
 
-    offsets = far_first(ysz, xsz)
+    offsets = even_chunks(ysz, xsz)
     own = ep_n - 1
 
     def peer(pos):
@@ -170,7 +148,7 @@
 
     for dz in range(1, PLANES):
         line_copy(dz, gsend, gz, gsend_sem.at[0], grecv_sem.at[0]).start()
-    send_rows(0, plane)
+    send_rows(0, 2 * plane)
     recv[own] = send[own]
     gz[my_plane] = gsend[my_plane]
     wait_bytes(gz, PLANES - 1, grecv_sem.at[0])
@@ -181,7 +159,7 @@
 
     lax.fori_loop(1, plane, spread, 0)
     grecv[my_in] = gz[...]
-    send_rows(plane, own)
+    send_rows(2 * plane, own)
 
     for pos in range(ep_n):
         zt, it = peer(pos)

time: 66 us -> 60.2 us (0.912)
  the two profiles are of different devices: /device:TPU:2 before, /device:TPU:39 now
where the time goes in v9:
time: 60.2 us; the launch traced here: 60 us
  Pallas kernels  59.4 us (99%)
  between operations  0.64 us (1%)
    pallas_call x1, Pallas kernels, local_backward(): pl.pallas_call(functools.partial(layer_kernel, cfg), out_shape=results, i...  57.1 us
    pallas_call x1, Pallas kernels, local_backward(): pl.pallas_call(write_kernel, out_shape=results, in_specs=[vmem] * 5, out_...  2.29 us

profile of v9, /device:TPU:39, one launch (start us, length us, event | category | flops | bytes accessed | tf_op | source)
XLA Modules:
  0.0 60.0 jit_solution(10743369629396712643)
XLA Ops:
  0.6 57.1 %layer.1 = (bf16[64,1536]{1,0:T(8,128)(2,1)S(1)}, f32[6,64]{1,0:T(8,128)S(1)}, f32[768,512]{1,0:T(8,128)S(1)}, f32[256,1536]{1,0:T(8,128)S(1)}, f32[768,512]{1,0:T(8,128)S(1)}) custom-call(bf16[64,1536]{1,0:T(8,128)(2,1)} %go_in.1, s32[6,64]{1,0:T(8,128)} %bitcast.21, s32[6,64]{1,0:T(8,128)} %bitcast.22, f32[6,64]{1,0:T(8,128)} %bitcast.23, ...), custom_call_target="tpu_custom_call" | custom-call | tf_op jit(solution)/shard_map/layer/pallas_call | solution.py:331
  57.7 2.3 %write.1 = (bf16[64,1536]{1,0:T(8,128)(2,1)}, f32[6,64]{1,0:T(8,128)}, f32[768,512]{1,0:T(8,128)}, f32[256,1536]{1,0:T(8,128)}, f32[768,512]{1,0:T(8,128)}) custom-call(bf16[64,1536]{1,0:T(8,128)(2,1)S(1)} %get-tuple-element.15.refs_0_, f32[6,64]{1,0:T(8,128)S(1)} %get-tuple-element.16.refs_1_, f32[768,512]{1,0:T(8,128)S(1)} %get-tuple-element.17.refs_2_, ...), custom_call_target="tpu_custom_call" | custom-call | tf_op jit(solution)/shard_map/write/pallas_call | solution.py:350

commit v10 on v9

--- a/solution.py
+++ b/solution.py
@@ -11,6 +11,7 @@
 F32 = jnp.float32
 BF16 = jnp.bfloat16
 PLANES = 4
+WRITE_PARTS = 4
 NT = (((1,), (1,)), ((), ()))
 TN = (((0,), (0,)), ((), ()))
 
@@ -55,11 +56,12 @@
 
     barrier = pltpu.get_barrier_semaphore()
 
-    def announce(o, c):
-        pl.semaphore_signal(barrier, inc=1, device_id=(q, lax.rem(me + o, ep_n)), device_id_type=MESH)
-        return c
-
-    lax.fori_loop(1, ep_n, announce, 0)
+    def hops(pos):
+        return sum(min(k, n - k) for k, n in zip(offsets[pos], (PLANES, ysz, xsz)))
+
+    for pos in sorted(range(own), key=lambda p: -hops(p)):
+        zt, it = peer(pos)
+        pl.semaphore_signal(barrier, inc=1, device_id=(q, zt * plane + it), device_id_type=MESH)
     pl.semaphore_signal(barrier, inc=1, device_id=(other, me), device_id_type=MESH)
 
     small = [
@@ -264,20 +266,21 @@
         mine_ref[...] += got[...]
 
     wait_bytes(back4, PLANES - 1, vrecv_sem.at[1])
+    vals = [jnp.zeros((lanes, tok_n), F32) for _ in range(top)]
+    for zp in range(PLANES):
+        back = jnp.sum(jnp.where(diag, back4[zp], 0.0), axis=1, keepdims=True)
+        for j in range(top):
+            hit = slot_s == dest[j:j + 1, :] - zp * lanes
+            vals[j] = jnp.where(hit, back, vals[j])
+    for j in range(top):
+        gg[j:j + 1, :] = jnp.sum(vals[j], axis=0, keepdims=True)
     acc = jnp.zeros((tok_n, width), F32)
-    vals = [jnp.zeros((lanes, tok_n), F32) for _ in range(top)]
     for zp in range(PLANES):
         wait_bytes(dxr, in_chunk(zp), brecv_sem.at[zp])
         blocks = pl.ds(zp * plane, plane)
         part = dxr[blocks].astype(F32).reshape(rows_chunk, width).astype(BF16)
         acc = acc + lax.dot_general(onehot[zp], part, TN, preferred_element_type=F32)
-        back = jnp.sum(jnp.where(diag, back4[zp], 0.0), axis=1, keepdims=True)
-        for j in range(top):
-            hit = slot_s == dest[j:j + 1, :] - zp * lanes
-            vals[j] = jnp.where(hit, back, vals[j])
     gx[...] = acc.astype(BF16)
-    for j in range(top):
-        gg[j:j + 1, :] = jnp.sum(vals[j], axis=0, keepdims=True)
 
     wait_bytes(send, ep_n - 1, fsend_sem)
     wait_bytes(gz, PLANES - 1, gsend_sem.at[0])
@@ -290,7 +293,13 @@
 def write_kernel(*refs):
     n = len(refs) // 2
     sem = refs[-1]
-    copies = [pltpu.make_async_copy(refs[i], refs[n + i], sem.at[i]) for i in range(n)]
+    copies = []
+    for i in range(n):
+        rows = refs[i].shape[0]
+        parts = WRITE_PARTS if rows % (8 * WRITE_PARTS) == 0 else 1
+        for p in range(parts):
+            part = pl.ds(p * (rows // parts), rows // parts)
+            copies.append(pltpu.make_async_copy(refs[i].at[part], refs[n + i].at[part], sem.at[i, p]))
     for cp in copies:
         cp.start()
     for cp in copies:
@@ -352,7 +361,7 @@
             out_shape=results,
             in_specs=[vmem] * 5,
             out_specs=[hbm] * 5,
-            scratch_shapes=[dma((5,))],
+            scratch_shapes=[dma((5, WRITE_PARTS))],
             compiler_params=pltpu.CompilerParams(vmem_limit_bytes=8 * 1024 * 1024),
             name='write',
         )(*outs)

time: 60.2 us -> 60.3 us (level)
  the two profiles are of different devices: /device:TPU:39 before, /device:TPU:17 now
where the time goes in v10:
time: 60.3 us; the launch traced here: 60.1 us
  Pallas kernels  59.4 us (99%)
  between operations  0.64 us (1%)
    pallas_call x1, Pallas kernels, local_backward(): pl.pallas_call(functools.partial(layer_kernel, cfg), out_shape=results, i...  57 us
    pallas_call x1, Pallas kernels, local_backward(): pl.pallas_call(write_kernel, out_shape=results, in_specs=[vmem] * 5, out_...  2.41 us

profile of v10, /device:TPU:17, one launch (start us, length us, event | category | flops | bytes accessed | tf_op | source)
XLA Modules:
  0.0 60.1 jit_solution(15316432924743808220)
XLA Ops:
  0.6 57.0 %layer.1 = (bf16[64,1536]{1,0:T(8,128)(2,1)S(1)}, f32[6,64]{1,0:T(8,128)S(1)}, f32[768,512]{1,0:T(8,128)S(1)}, f32[256,1536]{1,0:T(8,128)S(1)}, f32[768,512]{1,0:T(8,128)S(1)}) custom-call(bf16[64,1536]{1,0:T(8,128)(2,1)} %go_in.1, s32[6,64]{1,0:T(8,128)} %bitcast.21, s32[6,64]{1,0:T(8,128)} %bitcast.22, f32[6,64]{1,0:T(8,128)} %bitcast.23, ...), custom_call_target="tpu_custom_call" | custom-call | tf_op jit(solution)/shard_map/layer/pallas_call | solution.py:340
  57.7 2.4 %write.1 = (bf16[64,1536]{1,0:T(8,128)(2,1)}, f32[6,64]{1,0:T(8,128)}, f32[768,512]{1,0:T(8,128)}, f32[256,1536]{1,0:T(8,128)}, f32[768,512]{1,0:T(8,128)}) custom-call(bf16[64,1536]{1,0:T(8,128)(2,1)S(1)} %get-tuple-element.15.refs_0_, f32[6,64]{1,0:T(8,128)S(1)} %get-tuple-element.16.refs_1_, f32[768,512]{1,0:T(8,128)S(1)} %get-tuple-element.17.refs_2_, ...), custom_call_target="tpu_custom_call" | custom-call | tf_op jit(solution)/shard_map/write/pallas_call | solution.py:359
